TPU v7x, 512 devices: a whole 4x8x8 slice. The times are simulated.
512 devices in a mesh: grp: 8 (over y), row: 64 (over z, x, core).
Axes of the slice: x: 4, y: 8, z: 8, core: 2. Of those that a mesh axis runs over, the one named last changes fastest.
Arguments:
- right_side: float32 [64, 65536], P(None, ('grp', 'row')), may hold values from -60 to 60
- links: int32 [8, 65536], P(None, ('grp', 'row')), may hold values from 0 to 65535, as said below
- coefs: float32 [65536], P(('grp', 'row')), may hold values from 0.3 to 3
- reaction: float32 [65536], P(('grp', 'row')), may hold values from 0.05 to 0.5
Outputs:
- solution: float32 [64, 65536], P(None, ('grp', 'row'))
- resid_rms: float32 [2, 64], replicated
Inputs may be any that keep to these rules, and one draw needn't show every extreme that they name: `links`: the nodes form a periodic grid of 32 x 128 x 16. Block (p, q), p < 8, q < 64, holds the nodes of first coordinate p * 4 to p * 4 + 3 and second coordinate q * 2 to q * 2 + 1, and these carry the unknowns and elements b * 4 * 2 * 16 to (b + 1) * 4 * 2 * 16 - 1, with b = p * 64 + q. Element b * 4 * 2 * 16 + (i * 2 + j) * 16 + k has its base at the node (p * 4 + i, q * 2 + j, k), and its corner l lies at the base plus (l mod 2, l // 2 mod 2, l // 4), modulo the grid. Within a block the unknowns are numbered in some order. Every unknown is a corner of 8 elements.
All inputs are finite; a program needn't handle non-finite values.
Results may differ from a plain program's by a relative error of at most 0.0003.
Values sent between devices are 32-bit elements; how exact they have to be, the bound alone decides.
No kernel may reach another device: no remote copies, remote signals or barrier semaphores. Data moves between devices by JAX's collectives and lax.ppermute only.
A program may use at most 64 MiB of HBM per device.

v0:
```python
import functools
import math

import jax
import jax.numpy as jnp
import numpy as np
from jax import lax
from jax.sharding import Mesh
from jax.sharding import PartitionSpec as P

SWEEPS = 2
DEGREE = 4
ROW = ("row_0", "row_1", "row_2")
GRP_ROW = ("grp", "row_0", "row_1", "row_2")


def shifted(block, axis, distance):
    devices = range(lax.axis_size(axis))
    route = [((i - distance) % len(devices), i) for i in devices]
    return lax.ppermute(block, axis, route)


def over_axes(array, axes):
    return functools.reduce(lax.psum, axes, array)


def element_matrix():
    node_ids = np.arange(8)
    corner = np.stack([node_ids % 2, node_ids // 2 % 2, node_ids // 4], axis=1)
    gauss_points = np.array([0.5 - 0.5 / math.sqrt(3.0), 0.5 + 0.5 / math.sqrt(3.0)])
    stiffness = np.zeros((8, 8))
    for q in range(8):
        quad_point = gauss_points[np.array([q % 2, q // 2 % 2, q // 4])]
        values = np.where(corner > 0.5, quad_point, 1.0 - quad_point)
        slopes = np.where(corner > 0.5, 1.0, -1.0)
        gradient = np.stack(
            [
                slopes[:, 0] * values[:, 1] * values[:, 2],
                values[:, 0] * slopes[:, 1] * values[:, 2],
                values[:, 0] * values[:, 1] * slopes[:, 2],
            ],
            axis=1,
        )
        stiffness = stiffness + gradient @ gradient.T / 8.0
    return stiffness


def element_images(window, offsets, weights, stiffness):
    corners = window[:, offsets]
    images = (
        jnp.einsum("ml,rle->rme", stiffness, corners, precision=lax.Precision.HIGHEST) * weights
    )
    return jnp.zeros_like(window).at[:, offsets].add(images)


def on_device(right_side, links, coefs, reaction):
    stiffness = jnp.asarray(element_matrix(), dtype=jnp.float32)
    count = right_side.shape[1]
    groups = lax.axis_size("grp")
    rowcount = lax.axis_size(ROW)
    group_id = lax.axis_index("grp")
    row_id = lax.axis_index(ROW)
    total = count * groups * rowcount
    owner = links // count
    slot = links % count
    first = jnp.mod(owner // rowcount - group_id, groups)
    second = jnp.mod(owner % rowcount - row_id, rowcount)
    offsets = (first * 2 + second) * count + slot

    def apply_operator(field):
        above_row = shifted(field, ROW, -1)
        upper = shifted(jnp.stack([field, above_row], axis=0), "grp", -1)
        window = jnp.concatenate([field, above_row, upper[0], upper[1]], axis=1)
        summed = element_images(window, offsets, coefs, stiffness)
        back = shifted(
            jnp.stack([summed[:, 2 * count : 3 * count], summed[:, 3 * count :]], axis=0), "grp", 1
        )
        first_col = summed[:, :count] + back[0]
        second_col = summed[:, count : 2 * count] + back[1]
        first_col = first_col + shifted(second_col, ROW, 1)
        return first_col + reaction * field

    image = apply_operator(right_side)
    cross, square = (
        over_axes(jnp.sum(right_side * image, axis=1), GRP_ROW),
        over_axes(jnp.sum(image * image, axis=1), GRP_ROW),
    )
    theta = square / cross
    upper = (1.5 * theta)[:, None]
    lower = upper / 10.0
    center = (upper + lower) / 2.0
    half = (upper - lower) / 2.0
    sigma = center / half
    solution = jnp.zeros_like(right_side)
    residual = right_side
    history = []
    for sweep in range(SWEEPS):
        start = residual
        correction = jnp.zeros_like(right_side)
        rho_now = 1.0 / sigma
        direction = residual / center
        for step in range(DEGREE):
            correction = correction + direction
            residual = residual - apply_operator(direction)
            if step + 1 < DEGREE:
                rho_next = 1.0 / (2.0 * sigma - rho_now)
                direction = rho_next * rho_now * direction + 2.0 * rho_next / half * residual
                rho_now = rho_next
        change = start - residual
        along, length, begin = (
            over_axes(jnp.sum(start * change, axis=1), GRP_ROW),
            over_axes(jnp.sum(change * change, axis=1), GRP_ROW),
            over_axes(jnp.sum(start * start, axis=1), GRP_ROW),
        )
        omega = along / length
        residual = start - omega[:, None] * change
        squares = begin - 2.0 * omega * along + omega * omega * length
        solution = solution + omega[:, None] * correction
        history.append(jnp.sqrt(squares / total))
    return (solution, jnp.stack(history, axis=0))


def solution(mesh):
    finer = Mesh(
        mesh.devices.reshape(mesh.shape["grp"], 8, 4, 2), ("grp", "row_0", "row_1", "row_2")
    )
    placed = (P(None, GRP_ROW), P(None, GRP_ROW), P(GRP_ROW), P(GRP_ROW))
    return jax.shard_map(
        on_device, mesh=finer, in_specs=placed, out_specs=(P(None, GRP_ROW), P()), check_vma=False
    )
```

profile of v0, /device:TPU:1, one launch (start us, length us, event | category | flops | bytes accessed | tf_op | source)
XLA Modules:
  0.0 480.9 jit_solution(6675358322546604341)
XLA Ops:
  1.5 8.7 %collective-permute-start = (f32[64,128]{0,1:T(8,128)S(1)}, f32[64,128]{0,1:T(8,128)S(1)}, u32[]{:S(2)}, u32[]{:S(2)}) collective-permute-start(f32[64,128]{0,1:T(8,128)S(1)} %copy.25), channel_id=1, source_target_pairs={{1,0},{2,1},{3,2},{4,3},{5,4},{6,5},{7,6},{8,7},{9,8},{10,9},{11,1... | collective-permute-start | bytes 98312 | tf_op jit(solution)/shard_map/ppermute | solution.py:20
  38.4 8.4 %collective-permute-done.3 = f32[64,128]{0,1:T(8,128)S(1)} collective-permute-done((f32[64,128]{0,1:T(8,128)S(1)}, f32[64,128]{0,1:T(8,128)S(1)}, u32[]{:S(2)}, u32[]{:S(2)}) %collective-permute-start.3) | collective-permute-done | bytes 32800 | tf_op jit(solution)/shard_map/ppermute | solution.py:20
  46.9 12.7 %all-reduce.5 = (f32[64]{0:T(128)S(1)}, f32[64]{0:T(128)S(1)}) all-reduce(f32[64]{0:T(128)S(1)} %get-tuple-element.10, f32[64]{0:T(128)S(1)} %get-tuple-element.9), channel_id=1, replica_groups=mesh['grp'=8,'row_0'=8,'row_1'=4,'row_2'=2] {'grp'}, use_global_device_ids=true, to_apply=%region_2.3 | all-reduce | flops 128 | bytes 1024 | tf_op jit(solution)/shard_map/psum | solution.py:24
  59.6 11.8 %all-reduce.2 = (f32[64]{0:T(128)S(1)}, f32[64]{0:T(128)S(1)}) all-reduce(f32[64]{0:T(128)S(1)} %get-tuple-element.25, f32[64]{0:T(128)S(1)} %get-tuple-element.26), channel_id=1, replica_groups=mesh['grp'=8,'row_0'=8,'row_1'=4,'row_2'=2] {'row_0'}, use_global_device_ids=true, to_apply=%region_3.4 | all-reduce | flops 128 | bytes 1024 | tf_op jit(solution)/shard_map/psum | solution.py:24
  71.4 10.4 %all-reduce.8 = (f32[64]{0:T(128)S(1)}, f32[64]{0:T(128)S(1)}) all-reduce(f32[64]{0:T(128)S(1)} %get-tuple-element.17, f32[64]{0:T(128)S(1)} %get-tuple-element.18), channel_id=1, replica_groups=mesh['grp'=8,'row_0'=8,'row_1'=4,'row_2'=2] {'row_1'}, use_global_device_ids=true, to_apply=%region_4.5 | all-reduce | flops 128 | bytes 1024 | tf_op jit(solution)/shard_map/psum | solution.py:24
  81.8 11.5 %all-reduce.11 = (f32[64]{0:T(128)S(1)}, f32[64]{0:T(128)S(1)}) all-reduce(f32[64]{0:T(128)S(1)} %get-tuple-element.33, f32[64]{0:T(128)S(1)} %get-tuple-element.34), channel_id=1, replica_groups=mesh['grp'=8,'row_0'=8,'row_1'=4,'row_2'=2] {'row_2'}, use_global_device_ids=true, to_apply=%region_5.6 | all-reduce | flops 128 | bytes 1024 | tf_op jit(solution)/shard_map/psum | solution.py:24
  108.5 6.1 %scatter_custom_fusion.1 = f32[64,512]{0,1:T(8,128)S(1)} fusion(s32[1024]{0:T(1024)S(1)} %get-tuple-element.64, f32[1024,64]{1,0:T(8,128)S(1)} %bitcast.333, f32[]{:T(128)} %constant.86.clone.1), kind=kCustom, calls=%fused_computation.86 | custom fusion | flops 65536 | bytes 131076 | tf_op jit(solution)/shard_map/scatter-add | solution.py:53
  128.8 7.5 %collective-permute-start.8 = (f32[64,128]{0,1:T(8,128)S(1)}, f32[64,128]{0,1:T(8,128)S(1)}, u32[]{:S(2)}, u32[]{:S(2)}) collective-permute-start(f32[64,128]{0,1:T(8,128)S(1)} %multiply_add_fusion.6), channel_id=1, source_target_pairs={{1,0},{2,1},{3,2},{4,3},{5,4},{6,5},{7,6},{8,7},{9,8},{10,9},{11,1... | collective-permute-start | bytes 98312 | tf_op jit(solution)/shard_map/ppermute | solution.py:20
  165.8 8.2 %collective-permute-start.12 = (f32[64,128]{0,1:T(8,128)S(1)}, f32[64,128]{0,1:T(8,128)S(1)}, u32[]{:S(2)}, u32[]{:S(2)}) collective-permute-start(f32[64,128]{0,1:T(8,128)S(1)} %get-tuple-element.59), channel_id=1, source_target_pairs={{1,0},{2,1},{3,2},{4,3},{5,4},{6,5},{7,6},{8,7},{9,8},{10,9},{11,1... | collective-permute-start | bytes 98312 | tf_op jit(solution)/shard_map/ppermute | solution.py:20
  203.3 8.2 %collective-permute-start.16 = (f32[64,128]{0,1:T(8,128)S(1)}, f32[64,128]{0,1:T(8,128)S(1)}, u32[]{:S(2)}, u32[]{:S(2)}) collective-permute-start(f32[64,128]{0,1:T(8,128)S(1)} %get-tuple-element.52), channel_id=1, source_target_pairs={{1,0},{2,1},{3,2},{4,3},{5,4},{6,5},{7,6},{8,7},{9,8},{10,9},{11,1... | collective-permute-start | bytes 98312 | tf_op jit(solution)/shard_map/ppermute | solution.py:20
  221.7 6.1 %scatter_custom_fusion.4 = f32[64,512]{0,1:T(8,128)S(1)} fusion(s32[1024]{0:T(1024)S(1)} %get-tuple-element.64, f32[1024,64]{1,0:T(8,128)S(1)} %bitcast.336, f32[]{:T(128)} %constant.86.clone.1), kind=kCustom, calls=%fused_computation.80 | custom fusion | flops 65536 | bytes 131076 | tf_op jit(solution)/shard_map/scatter-add | solution.py:53
  240.9 11.5 %all-reduce.4 = (f32[64]{0:T(128)S(1)}, f32[64]{0:T(128)S(1)}) all-reduce(f32[64]{0:T(128)S(1)} %get-tuple-element.8, f32[64]{0:T(128)S(1)} %get-tuple-element.7), channel_id=1, replica_groups=mesh['grp'=8,'row_0'=8,'row_1'=4,'row_2'=2] {'grp'}, use_global_device_ids=true, to_apply=%region_16.17 | all-reduce | flops 128 | bytes 1024 | tf_op jit(solution)/shard_map/psum | solution.py:24
  252.4 10.7 %all-reduce.1 = (f32[64]{0:T(128)S(1)}, f32[64]{0:T(128)S(1)}) all-reduce(f32[64]{0:T(128)S(1)} %get-tuple-element.23, f32[64]{0:T(128)S(1)} %get-tuple-element.24), channel_id=1, replica_groups=mesh['grp'=8,'row_0'=8,'row_1'=4,'row_2'=2] {'row_0'}, use_global_device_ids=true, to_apply=%region_17.18 | all-reduce | flops 128 | bytes 1024 | tf_op jit(solution)/shard_map/psum | solution.py:24
  263.0 11.5 %all-reduce.7 = (f32[64]{0:T(128)S(1)}, f32[64]{0:T(128)S(1)}) all-reduce(f32[64]{0:T(128)S(1)} %get-tuple-element.15, f32[64]{0:T(128)S(1)} %get-tuple-element.16), channel_id=1, replica_groups=mesh['grp'=8,'row_0'=8,'row_1'=4,'row_2'=2] {'row_1'}, use_global_device_ids=true, to_apply=%region_18.19 | all-reduce | flops 128 | bytes 1024 | tf_op jit(solution)/shard_map/psum | solution.py:24
  274.6 11.5 %all-reduce.10 = (f32[64]{0:T(128)S(1)}, f32[64]{0:T(128)S(1)}) all-reduce(f32[64]{0:T(128)S(1)} %get-tuple-element.31, f32[64]{0:T(128)S(1)} %get-tuple-element.32), channel_id=1, replica_groups=mesh['grp'=8,'row_0'=8,'row_1'=4,'row_2'=2] {'row_2'}, use_global_device_ids=true, to_apply=%region_19.20 | all-reduce | flops 128 | bytes 1024 | tf_op jit(solution)/shard_map/psum | solution.py:24
  321.6 7.5 %collective-permute-start.24 = (f32[64,128]{0,1:T(8,128)S(1)}, f32[64,128]{0,1:T(8,128)S(1)}, u32[]{:S(2)}, u32[]{:S(2)}) collective-permute-start(f32[64,128]{0,1:T(8,128)S(1)} %multiply_add_fusion.3), channel_id=1, source_target_pairs={{1,0},{2,1},{3,2},{4,3},{5,4},{6,5},{7,6},{8,7},{9,8},{10,9},{11,1... | collective-permute-start | bytes 98312 | tf_op jit(solution)/shard_map/ppermute | solution.py:20
  339.4 6.3 %scatter_custom_fusion.6 = f32[64,512]{0,1:T(8,128)S(1)} fusion(s32[1024]{0:T(1024)S(1)} %get-tuple-element.64, f32[1024,64]{1,0:T(8,128)S(1)} %bitcast.338, f32[]{:T(128)} %constant.86.clone.1), kind=kCustom, calls=%fused_computation.76 | custom fusion | flops 65536 | bytes 131076 | tf_op jit(solution)/shard_map/scatter-add | solution.py:53
  358.8 8.2 %collective-permute-start.28 = (f32[64,128]{0,1:T(8,128)S(1)}, f32[64,128]{0,1:T(8,128)S(1)}, u32[]{:S(2)}, u32[]{:S(2)}) collective-permute-start(f32[64,128]{0,1:T(8,128)S(1)} %get-tuple-element.47), channel_id=1, source_target_pairs={{1,0},{2,1},{3,2},{4,3},{5,4},{6,5},{7,6},{8,7},{9,8},{10,9},{11,1... | collective-permute-start | bytes 98312 | tf_op jit(solution)/shard_map/ppermute | solution.py:20
  377.2 6.1 %scatter_custom_fusion.7 = f32[64,512]{0,1:T(8,128)S(1)} fusion(s32[1024]{0:T(1024)S(1)} %get-tuple-element.64, f32[1024,64]{1,0:T(8,128)S(1)} %bitcast.339, f32[]{:T(128)} %constant.86.clone.1), kind=kCustom, calls=%fused_computation.74 | custom fusion | flops 65536 | bytes 131076 | tf_op jit(solution)/shard_map/scatter-add | solution.py:53
  396.3 8.2 %collective-permute-start.32 = (f32[64,128]{0,1:T(8,128)S(1)}, f32[64,128]{0,1:T(8,128)S(1)}, u32[]{:S(2)}, u32[]{:S(2)}) collective-permute-start(f32[64,128]{0,1:T(8,128)S(1)} %get-tuple-element.45), channel_id=1, source_target_pairs={{1,0},{2,1},{3,2},{4,3},{5,4},{6,5},{7,6},{8,7},{9,8},{10,9},{11,1... | collective-permute-start | bytes 98312 | tf_op jit(solution)/shard_map/ppermute | solution.py:20
  433.9 12.0 %all-reduce.3 = (f32[64]{0:T(128)S(1)}, f32[64]{0:T(128)S(1)}, f32[64]{0:T(128)S(1)}, f32[64]{0:T(128)S(1)}) all-reduce(f32[64]{0:T(128)S(1)} %get-tuple-element.5, f32[64]{0:T(128)S(1)} %get-tuple-element.6, f32[64]{0:T(128)S(1)} %get-tuple-element.4, ...), channel_id=1, replica_groups=mesh['grp'=8,'row_0'=8,'row_1'=4,'row_2'=2] {'grp'}, use_global_device_ids=true, to_apply=%region_30.31 | all-reduce | flops 256 | bytes 2048 | tf_op jit(solution)/shard_map/psum | solution.py:24
  445.9 10.7 %all-reduce = (f32[64]{0:T(128)S(1)}, f32[64]{0:T(128)S(1)}, f32[64]{0:T(128)S(1)}, f32[64]{0:T(128)S(1)}) all-reduce(f32[64]{0:T(128)S(1)} %get-tuple-element.19, f32[64]{0:T(128)S(1)} %get-tuple-element.20, f32[64]{0:T(128)S(1)} %get-tuple-element.21, ...), channel_id=1, replica_groups=mesh['grp'=8,'row_0'=8,'row_1'=4,'row_2'=2] {'row_0'}, use_global_device_ids=true, to_apply=%region_31.32 | all-reduce | flops 256 | bytes 2048 | tf_op jit(solution)/shard_map/psum | solution.py:24
  456.6 11.4 %all-reduce.6 = (f32[64]{0:T(128)S(1)}, f32[64]{0:T(128)S(1)}, f32[64]{0:T(128)S(1)}, f32[64]{0:T(128)S(1)}) all-reduce(f32[64]{0:T(128)S(1)} %get-tuple-element.11, f32[64]{0:T(128)S(1)} %get-tuple-element.12, f32[64]{0:T(128)S(1)} %get-tuple-element.13, ...), channel_id=1, replica_groups=mesh['grp'=8,'row_0'=8,'row_1'=4,'row_2'=2] {'row_1'}, use_global_device_ids=true, to_apply=%region_32.33 | all-reduce | flops 256 | bytes 2048 | tf_op jit(solution)/shard_map/psum | solution.py:24
  468.0 11.5 %all-reduce.9 = (f32[64]{0:T(128)S(1)}, f32[64]{0:T(128)S(1)}, f32[64]{0:T(128)S(1)}, f32[64]{0:T(128)S(1)}) all-reduce(f32[64]{0:T(128)S(1)} %get-tuple-element.27, f32[64]{0:T(128)S(1)} %get-tuple-element.28, f32[64]{0:T(128)S(1)} %get-tuple-element.29, ...), channel_id=1, replica_groups=mesh['grp'=8,'row_0'=8,'row_1'=4,'row_2'=2] {'row_2'}, use_global_device_ids=true, to_apply=%region_33.34 | all-reduce | flops 256 | bytes 2048 | tf_op jit(solution)/shard_map/psum | solution.py:24
  (191 shorter events, 252.5 us)
Async XLA Ops:
  1.5 9.6 %collective-permute-start = (f32[64,128]{0,1:T(8,128)S(1)}, f32[64,128]{0,1:T(8,128)S(1)}, u32[]{:S(2)}, u32[]{:S(2)}) collective-permute-start(f32[64,128]{0,1:T(8,128)S(1)} %copy.25), channel_id=1, source_target_pairs={{1,0},{2,1},{3,2},{4,3},{5,4},{6,5},{7,6},{8,7},{9,8},{10,9},{11,1... | collective-permute-start | bytes 98312 | tf_op jit(solution)/shard_map/ppermute | solution.py:20
  27.1 6.9 %collective-permute-start.2 = (f32[2,64,128]{1,2,0:T(8,128)S(1)}, f32[2,64,128]{1,2,0:T(8,128)S(1)}, u32[]{:S(2)}, u32[]{:S(2)}) collective-permute-start(f32[2,64,128]{1,2,0:T(8,128)S(1)} %pad_maximum_fusion.10), channel_id=1, source_target_pairs={{448,0},{0,64},{64,128},{128,192},{192,256},{256,320},{320,384},{3... | collective-permute-start | bytes 196616 | tf_op jit(solution)/shard_map/ppermute | solution.py:20
  34.1 12.7 %collective-permute-start.3 = (f32[64,128]{0,1:T(8,128)S(1)}, f32[64,128]{0,1:T(8,128)S(1)}, u32[]{:S(2)}, u32[]{:S(2)}) collective-permute-start(f32[64,128]{0,1:T(8,128)S(1)} %fusion.78), channel_id=1, source_target_pairs={{63,0},{0,1},{1,2},{2,3},{3,4},{4,5},{5,6},{6,7},{7,8},{8,9},{9,10... | collective-permute-start | bytes 98312 | tf_op jit(solution)/shard_map/ppermute | solution.py:20
  114.7 6.9 %collective-permute-start.6 = (f32[2,64,128]{1,2,0:T(8,128)S(1)}, f32[2,64,128]{1,2,0:T(8,128)S(1)}, u32[]{:S(2)}, u32[]{:S(2)}) collective-permute-start(f32[2,64,128]{1,2,0:T(8,128)S(1)} %pad_maximum_fusion.12), channel_id=1, source_target_pairs={{448,0},{0,64},{64,128},{128,192},{192,256},{256,320},{320,384},{3... | collective-permute-start | bytes 196616 | tf_op jit(solution)/shard_map/ppermute | solution.py:20
  121.6 7.1 %collective-permute-start.7 = (f32[64,128]{0,1:T(8,128)S(1)}, f32[64,128]{0,1:T(8,128)S(1)}, u32[]{:S(2)}, u32[]{:S(2)}) collective-permute-start(f32[64,128]{0,1:T(8,128)S(1)} %fusion.73), channel_id=1, source_target_pairs={{63,0},{0,1},{1,2},{2,3},{3,4},{4,5},{5,6},{6,7},{7,8},{8,9},{9,10... | collective-permute-start | bytes 98312 | tf_op jit(solution)/shard_map/ppermute | solution.py:20
  128.8 8.4 %collective-permute-start.8 = (f32[64,128]{0,1:T(8,128)S(1)}, f32[64,128]{0,1:T(8,128)S(1)}, u32[]{:S(2)}, u32[]{:S(2)}) collective-permute-start(f32[64,128]{0,1:T(8,128)S(1)} %multiply_add_fusion.6), channel_id=1, source_target_pairs={{1,0},{2,1},{3,2},{4,3},{5,4},{6,5},{7,6},{8,7},{9,8},{10,9},{11,1... | collective-permute-start | bytes 98312 | tf_op jit(solution)/shard_map/ppermute | solution.py:20
  152.8 6.9 %collective-permute-start.10 = (f32[2,64,128]{1,2,0:T(8,128)S(1)}, f32[2,64,128]{1,2,0:T(8,128)S(1)}, u32[]{:S(2)}, u32[]{:S(2)}) collective-permute-start(f32[2,64,128]{1,2,0:T(8,128)S(1)} %pad_maximum_fusion.14), channel_id=1, source_target_pairs={{448,0},{0,64},{64,128},{128,192},{192,256},{256,320},{320,384},{3... | collective-permute-start | bytes 196616 | tf_op jit(solution)/shard_map/ppermute | solution.py:20
  159.7 6.0 %collective-permute-start.11 = (f32[64,128]{0,1:T(8,128)S(1)}, f32[64,128]{0,1:T(8,128)S(1)}, u32[]{:S(2)}, u32[]{:S(2)}) collective-permute-start(f32[64,128]{0,1:T(8,128)S(1)} %fusion.68), channel_id=1, source_target_pairs={{63,0},{0,1},{1,2},{2,3},{3,4},{4,5},{5,6},{6,7},{7,8},{8,9},{9,10... | collective-permute-start | bytes 98312 | tf_op jit(solution)/shard_map/ppermute | solution.py:20
  165.8 9.1 %collective-permute-start.12 = (f32[64,128]{0,1:T(8,128)S(1)}, f32[64,128]{0,1:T(8,128)S(1)}, u32[]{:S(2)}, u32[]{:S(2)}) collective-permute-start(f32[64,128]{0,1:T(8,128)S(1)} %get-tuple-element.59), channel_id=1, source_target_pairs={{1,0},{2,1},{3,2},{4,3},{5,4},{6,5},{7,6},{8,7},{9,8},{10,9},{11,1... | collective-permute-start | bytes 98312 | tf_op jit(solution)/shard_map/ppermute | solution.py:20
  190.3 6.9 %collective-permute-start.14 = (f32[2,64,128]{1,2,0:T(8,128)S(1)}, f32[2,64,128]{1,2,0:T(8,128)S(1)}, u32[]{:S(2)}, u32[]{:S(2)}) collective-permute-start(f32[2,64,128]{1,2,0:T(8,128)S(1)} %pad_maximum_fusion.16), channel_id=1, source_target_pairs={{448,0},{0,64},{64,128},{128,192},{192,256},{256,320},{320,384},{3... | collective-permute-start | bytes 196616 | tf_op jit(solution)/shard_map/ppermute | solution.py:20
  197.2 6.0 %collective-permute-start.15 = (f32[64,128]{0,1:T(8,128)S(1)}, f32[64,128]{0,1:T(8,128)S(1)}, u32[]{:S(2)}, u32[]{:S(2)}) collective-permute-start(f32[64,128]{0,1:T(8,128)S(1)} %fusion.63), channel_id=1, source_target_pairs={{63,0},{0,1},{1,2},{2,3},{3,4},{4,5},{5,6},{6,7},{7,8},{8,9},{9,10... | collective-permute-start | bytes 98312 | tf_op jit(solution)/shard_map/ppermute | solution.py:20
  203.3 9.1 %collective-permute-start.16 = (f32[64,128]{0,1:T(8,128)S(1)}, f32[64,128]{0,1:T(8,128)S(1)}, u32[]{:S(2)}, u32[]{:S(2)}) collective-permute-start(f32[64,128]{0,1:T(8,128)S(1)} %get-tuple-element.52), channel_id=1, source_target_pairs={{1,0},{2,1},{3,2},{4,3},{5,4},{6,5},{7,6},{8,7},{9,8},{10,9},{11,1... | collective-permute-start | bytes 98312 | tf_op jit(solution)/shard_map/ppermute | solution.py:20
  227.9 6.9 %collective-permute-start.18 = (f32[2,64,128]{1,2,0:T(8,128)S(1)}, f32[2,64,128]{1,2,0:T(8,128)S(1)}, u32[]{:S(2)}, u32[]{:S(2)}) collective-permute-start(f32[2,64,128]{1,2,0:T(8,128)S(1)} %pad_maximum_fusion.18), channel_id=1, source_target_pairs={{448,0},{0,64},{64,128},{128,192},{192,256},{256,320},{320,384},{3... | collective-permute-start | bytes 196616 | tf_op jit(solution)/shard_map/ppermute | solution.py:20
  234.8 6.0 %collective-permute-start.19 = (f32[64,128]{0,1:T(8,128)S(1)}, f32[64,128]{0,1:T(8,128)S(1)}, u32[]{:S(2)}, u32[]{:S(2)}) collective-permute-start(f32[64,128]{0,1:T(8,128)S(1)} %fusion.57), channel_id=1, source_target_pairs={{63,0},{0,1},{1,2},{2,3},{3,4},{4,5},{5,6},{6,7},{7,8},{8,9},{9,10... | collective-permute-start | bytes 98312 | tf_op jit(solution)/shard_map/ppermute | solution.py:20
  307.4 6.9 %collective-permute-start.22 = (f32[2,64,128]{1,2,0:T(8,128)S(1)}, f32[2,64,128]{1,2,0:T(8,128)S(1)}, u32[]{:S(2)}, u32[]{:S(2)}) collective-permute-start(f32[2,64,128]{1,2,0:T(8,128)S(1)} %pad_maximum_fusion.20), channel_id=1, source_target_pairs={{448,0},{0,64},{64,128},{128,192},{192,256},{256,320},{320,384},{3... | collective-permute-start | bytes 196616 | tf_op jit(solution)/shard_map/ppermute | solution.py:20
  314.4 7.1 %collective-permute-start.23 = (f32[64,128]{0,1:T(8,128)S(1)}, f32[64,128]{0,1:T(8,128)S(1)}, u32[]{:S(2)}, u32[]{:S(2)}) collective-permute-start(f32[64,128]{0,1:T(8,128)S(1)} %fusion.52), channel_id=1, source_target_pairs={{63,0},{0,1},{1,2},{2,3},{3,4},{4,5},{5,6},{6,7},{7,8},{8,9},{9,10... | collective-permute-start | bytes 98312 | tf_op jit(solution)/shard_map/ppermute | solution.py:20
  321.6 8.4 %collective-permute-start.24 = (f32[64,128]{0,1:T(8,128)S(1)}, f32[64,128]{0,1:T(8,128)S(1)}, u32[]{:S(2)}, u32[]{:S(2)}) collective-permute-start(f32[64,128]{0,1:T(8,128)S(1)} %multiply_add_fusion.3), channel_id=1, source_target_pairs={{1,0},{2,1},{3,2},{4,3},{5,4},{6,5},{7,6},{8,7},{9,8},{10,9},{11,1... | collective-permute-start | bytes 98312 | tf_op jit(solution)/shard_map/ppermute | solution.py:20
  345.8 6.9 %collective-permute-start.26 = (f32[2,64,128]{1,2,0:T(8,128)S(1)}, f32[2,64,128]{1,2,0:T(8,128)S(1)}, u32[]{:S(2)}, u32[]{:S(2)}) collective-permute-start(f32[2,64,128]{1,2,0:T(8,128)S(1)} %pad_maximum_fusion.22), channel_id=1, source_target_pairs={{448,0},{0,64},{64,128},{128,192},{192,256},{256,320},{320,384},{3... | collective-permute-start | bytes 196616 | tf_op jit(solution)/shard_map/ppermute | solution.py:20
  352.7 6.0 %collective-permute-start.27 = (f32[64,128]{0,1:T(8,128)S(1)}, f32[64,128]{0,1:T(8,128)S(1)}, u32[]{:S(2)}, u32[]{:S(2)}) collective-permute-start(f32[64,128]{0,1:T(8,128)S(1)} %fusion.47), channel_id=1, source_target_pairs={{63,0},{0,1},{1,2},{2,3},{3,4},{4,5},{5,6},{6,7},{7,8},{8,9},{9,10... | collective-permute-start | bytes 98312 | tf_op jit(solution)/shard_map/ppermute | solution.py:20
  358.8 9.1 %collective-permute-start.28 = (f32[64,128]{0,1:T(8,128)S(1)}, f32[64,128]{0,1:T(8,128)S(1)}, u32[]{:S(2)}, u32[]{:S(2)}) collective-permute-start(f32[64,128]{0,1:T(8,128)S(1)} %get-tuple-element.47), channel_id=1, source_target_pairs={{1,0},{2,1},{3,2},{4,3},{5,4},{6,5},{7,6},{8,7},{9,8},{10,9},{11,1... | collective-permute-start | bytes 98312 | tf_op jit(solution)/shard_map/ppermute | solution.py:20
  383.3 6.9 %collective-permute-start.30 = (f32[2,64,128]{1,2,0:T(8,128)S(1)}, f32[2,64,128]{1,2,0:T(8,128)S(1)}, u32[]{:S(2)}, u32[]{:S(2)}) collective-permute-start(f32[2,64,128]{1,2,0:T(8,128)S(1)} %pad_maximum_fusion.24), channel_id=1, source_target_pairs={{448,0},{0,64},{64,128},{128,192},{192,256},{256,320},{320,384},{3... | collective-permute-start | bytes 196616 | tf_op jit(solution)/shard_map/ppermute | solution.py:20
  390.3 6.0 %collective-permute-start.31 = (f32[64,128]{0,1:T(8,128)S(1)}, f32[64,128]{0,1:T(8,128)S(1)}, u32[]{:S(2)}, u32[]{:S(2)}) collective-permute-start(f32[64,128]{0,1:T(8,128)S(1)} %fusion.42), channel_id=1, source_target_pairs={{63,0},{0,1},{1,2},{2,3},{3,4},{4,5},{5,6},{6,7},{7,8},{8,9},{9,10... | collective-permute-start | bytes 98312 | tf_op jit(solution)/shard_map/ppermute | solution.py:20
  396.3 9.1 %collective-permute-start.32 = (f32[64,128]{0,1:T(8,128)S(1)}, f32[64,128]{0,1:T(8,128)S(1)}, u32[]{:S(2)}, u32[]{:S(2)}) collective-permute-start(f32[64,128]{0,1:T(8,128)S(1)} %get-tuple-element.45), channel_id=1, source_target_pairs={{1,0},{2,1},{3,2},{4,3},{5,4},{6,5},{7,6},{8,7},{9,8},{10,9},{11,1... | collective-permute-start | bytes 98312 | tf_op jit(solution)/shard_map/ppermute | solution.py:20
  420.9 6.9 %collective-permute-start.34 = (f32[2,64,128]{1,2,0:T(8,128)S(1)}, f32[2,64,128]{1,2,0:T(8,128)S(1)}, u32[]{:S(2)}, u32[]{:S(2)}) collective-permute-start(f32[2,64,128]{1,2,0:T(8,128)S(1)} %pad_maximum_fusion.26), channel_id=1, source_target_pairs={{448,0},{0,64},{64,128},{128,192},{192,256},{256,320},{320,384},{3... | collective-permute-start | bytes 196616 | tf_op jit(solution)/shard_map/ppermute | solution.py:20
  (16 other events, 111.2 us)
where the time goes:
time: 482 us; the launch traced here: 481 us
  blocking collectives  137 us (28%)
  starting transfers between devices  132 us (27%)
  waiting for transfers between devices  118 us (24%)
  other arithmetic  57.9 us (12%)
  local copies, waits for them, and re-layouts  31.2 us (6%)
    psum x12, blocking collectives, over_axes(): return functools.reduce(lax.psum, axes, array)  137 us
    ppermute x36, starting transfers between devices, shifted(): return lax.ppermute(block, axis, route)  132 us
    ppermute x36, waiting for transfers between devices, shifted(): return lax.ppermute(block, axis, route)  118 us
    scatter-add x9, other arithmetic, element_images(): return jnp.zeros_like(window).at[:, offsets].add(images)  55 us
    gather x18, local copies, waits for them, and re-layouts, element_images(): corners = window[:, offsets]  27.1 us
  transfers between devices with their start and end apart: 36, of which 36 were waited for; matrix products, arithmetic and copies ran while one was open for 0% of the time, Pallas kernels for 0%

commit v1 on v0

v1 whole, which is shorter than its diff:
```python
import jax
import jax.numpy as jnp
from jax import lax
from jax.experimental import pallas as pl
from jax.experimental.pallas import tpu as pltpu
from jax.sharding import Mesh
from jax.sharding import PartitionSpec as P

SWEEPS = 2
DEGREE = 4
HIGHEST = lax.Precision.HIGHEST


def dot(a, b, dims=((1,), (0,))):
    return lax.dot_general(a, b, (dims, ((), ())), precision=HIGHEST, preferred_element_type=jnp.float32)


def pack_kernel(right_ref, links_ref, coefs_ref, reaction_ref, message_ref, order_ref):
    row = lax.broadcasted_iota(jnp.int32, (128, 128), 0)
    lane = lax.broadcasted_iota(jnp.int32, (128, 128), 1)
    regroup = (row == (lane % 8) * 16 + lane // 8).astype(jnp.float32)
    slot = links_ref[0:1, :] & 127
    onehot = (row == slot).astype(jnp.float32)
    order = dot(onehot, regroup)
    order_ref[...] = order
    message_ref[:, 0:128] = dot(right_ref[...], order)
    coefs = dot(jnp.broadcast_to(coefs_ref[...], (8, 128)), regroup)
    reaction = dot(jnp.broadcast_to(reaction_ref[...], (8, 128)), order)
    for block in range(8):
        message_ref[block * 8 : block * 8 + 8, 128:256] = coefs
        message_ref[block * 8 : block * 8 + 8, 256:384] = reaction


def unpack_kernel(message_ref, order_ref, solution_ref, history_ref):
    solution_ref[...] = dot(message_ref[:, 0:128], order_ref[...], ((1,), (1,)))
    history_ref[...] = jnp.transpose(message_ref[:, 128:256])[0:8, :]


def exchange_lanes(tile):
    row = lax.broadcasted_iota(jnp.int32, (8, 128), 0)
    lane = lax.broadcasted_iota(jnp.int32, (8, 128), 1)
    for bit in (1, 2, 4):
        from_below = pltpu.roll(pltpu.roll(tile, 8 - bit, 0), bit, 1)
        from_above = pltpu.roll(pltpu.roll(tile, bit, 0), 128 - bit, 1)
        lane_bit = (lane & bit) != 0
        same = ((row & bit) != 0) == lane_bit
        tile = jnp.where(same, tile, jnp.where(lane_bit, from_below, from_above))
    return tile


def solve_kernel(
    parts_ref, out_ref, regroup_ref, shift_ref, direct_ref, turned_ref, residual_ref, start_ref,
    coef_ref, reaction_ref, minus_ref, plus_ref, correct_ref, solution_ref,
):
    lane = lax.broadcasted_iota(jnp.int32, (8, 128), 1)
    last_z = (lane & 7) == 7
    first_z = (lane & 7) == 0
    mine = lax.axis_index("x") * 2 + lax.axis_index("core")

    def next_z(v):
        return jnp.where(last_z, pltpu.roll(v, 7, 1), pltpu.roll(v, 127, 1))

    def prev_z(v):
        return jnp.where(first_z, pltpu.roll(v, 121, 1), pltpu.roll(v, 1, 1))

    def next_k(v):
        return pltpu.roll(v, 120, 1)

    def prev_k(v):
        return pltpu.roll(v, 8, 1)

    cells = [(i, w) for w in range(16) for i in range(4)]

    for kind in range(3):
        for x in range(4):
            for core in range(2):
                for y in range(8):
                    tile = parts_ref[core, x, y * 8 : y * 8 + 8, kind * 128 : kind * 128 + 128]
                    regroup_ref[x * 2 + core, y * 8 : y * 8 + 8, :] = exchange_lanes(tile)
        for i, w in cells:
            v = regroup_ref[w // 2, pl.ds(i * 2 + w % 2, 8, stride=8), :]
            if kind == 0:
                residual_ref[i, w] = v
                direct_ref[i, w] = v
                turned_ref[i, w] = next_k(v)
            elif kind == 1:
                coef_ref[0, i, w] = v * (1.0 / 16.0)
                coef_ref[1, i, w] = v * (1.0 / 24.0)
                coef_ref[2, i, w] = v * (1.0 / 48.0)
            else:
                reaction_ref[i, w] = v

    def halves(v, shifted):
        return v + shifted, shifted - v

    def next_i(vs):
        return [vs[1], vs[2], vs[3], pltpu.roll(vs[0], 7, 0)]

    def prev_i(vs):
        return [pltpu.roll(vs[3], 1, 0), vs[0], vs[1], vs[2]]

    def fold(minus_sum, sums):
        return [m + s for m, s in zip(minus_sum, prev_i(sums))]

    def apply_stiffness():
        def load(w):
            pairs = [halves(direct_ref[i, w], turned_ref[i, w]) for i in range(4)]
            return [p[0] for p in pairs], [p[1] for p in pairs]

        wrapped = []
        for i in range(4):
            v = next_z(direct_ref[i, 0])
            wrapped.append(halves(v, next_k(v)))
        wrapped = [p[0] for p in wrapped], [p[1] for p in wrapped]
        here = load(0)
        carry = None
        kept = None
        for w in range(16):
            there = load(w + 1) if w < 15 else wrapped
            grads = []
            for zk in range(2):
                for yk in range(2):
                    vs = [halves(a, b)[yk] for a, b in zip(here[zk], there[zk])]
                    nexts = next_i(vs)
                    differ = [(b - a) * coef_ref[zk + yk, i, w] for i, (a, b) in enumerate(zip(vs, nexts))]
                    if zk + yk:
                        total = [(a + b) * coef_ref[zk + yk - 1, i, w] for i, (a, b) in enumerate(zip(vs, nexts))]
                        grads.append(fold([s - d for s, d in zip(total, differ)], [s + d for s, d in zip(total, differ)]))
                    else:
                        grads.append(fold([-d for d in differ], differ))
            low = [[s - d for s, d in zip(grads[zk * 2], grads[zk * 2 + 1])] for zk in range(2)]
            high = [[s + d for s, d in zip(grads[zk * 2], grads[zk * 2 + 1])] for zk in range(2)]
            if w == 0:
                kept = low
            else:
                low = [[a + b for a, b in zip(low[zk], carry[zk])] for zk in range(2)]
                for i in range(4):
                    minus_ref[i, w] = low[0][i] - low[1][i]
                    plus_ref[i, w] = low[0][i] + low[1][i]
            carry = high
            here = there
        for i in range(4):
            s = kept[0][i] + prev_z(carry[0][i])
            d = kept[1][i] + prev_z(carry[1][i])
            minus_ref[i, 0] = s - d
            plus_ref[i, 0] = s + d

    def image_of(i, w, v):
        return minus_ref[i, w] + prev_k(plus_ref[i, w]) + reaction_ref[i, w] * v

    def over_all(v):
        return jnp.sum(jnp.sum(v, axis=1, keepdims=True), axis=0, keepdims=True)

    zero = jnp.zeros((8, 128), jnp.float32)

    apply_stiffness()
    crosses = [zero] * 4
    squares = [zero] * 4
    for i, w in cells:
        v = direct_ref[i, w]
        image = image_of(i, w, v)
        crosses[i] = crosses[i] + v * image
        squares[i] = squares[i] + image * image
    cross = over_all((crosses[0] + crosses[1]) + (crosses[2] + crosses[3]))
    square = over_all((squares[0] + squares[1]) + (squares[2] + squares[3]))
    theta = square / cross
    upper = 1.5 * theta
    lower = upper / 10.0
    center = (upper + lower) / 2.0
    half = (upper - lower) / 2.0
    sigma = center / half
    per_center = 1.0 / center

    for sweep in range(SWEEPS):
        scale = jnp.broadcast_to(per_center, (8, 128))
        for i, w in cells:
            r = residual_ref[i, w]
            start_ref[i, w] = r
            v = r * scale
            direct_ref[i, w] = v
            turned_ref[i, w] = next_k(v)
        for ij in range(8):
            correct_ref[ij] = zero

        def step(_, rho_now):
            for ij in range(8):
                correct_ref[ij] = correct_ref[ij] + direct_ref[ij // 2, mine * 2 + ij % 2]
            apply_stiffness()
            rho_next = 1.0 / (2.0 * sigma - rho_now)
            along = jnp.broadcast_to(rho_next * rho_now, (8, 128))
            across = jnp.broadcast_to(2.0 * rho_next / half, (8, 128))
            for i, w in cells:
                v = direct_ref[i, w]
                r = residual_ref[i, w] - image_of(i, w, v)
                residual_ref[i, w] = r
                v = along * v + across * r
                direct_ref[i, w] = v
                turned_ref[i, w] = next_k(v)
            return rho_next

        lax.fori_loop(0, DEGREE, step, 1.0 / sigma)
        crosses = [zero] * 4
        squares = [zero] * 4
        for i, w in cells:
            s = start_ref[i, w]
            change = s - residual_ref[i, w]
            crosses[i] = crosses[i] + s * change
            squares[i] = squares[i] + change * change
        along = over_all((crosses[0] + crosses[1]) + (crosses[2] + crosses[3]))
        length = over_all((squares[0] + squares[1]) + (squares[2] + squares[3]))
        omega = jnp.broadcast_to(along / length, (8, 128))
        squares = [zero] * 4
        for i, w in cells:
            s = start_ref[i, w]
            r = s - omega * (s - residual_ref[i, w])
            residual_ref[i, w] = r
            squares[i] = squares[i] + r * r
        for ij in range(8):
            if sweep == 0:
                solution_ref[ij] = omega * correct_ref[ij]
            else:
                solution_ref[ij] = solution_ref[ij] + omega * correct_ref[ij]
        total = over_all((squares[0] + squares[1]) + (squares[2] + squares[3]))
        rms = jnp.broadcast_to(jnp.sqrt(total / 65536.0), (8, 128))
        if sweep == 0:
            history = rms
        else:
            history = jnp.where(lane == sweep, rms, history)

    for ij in range(8):
        shift_ref[pl.ds(ij, 8, stride=8), :] = solution_ref[ij]
    for y in range(8):
        out_ref[y * 8 : y * 8 + 8, 0:128] = exchange_lanes(shift_ref[y * 8 : y * 8 + 8, :])
        out_ref[y * 8 : y * 8 + 8, 128:256] = history


def field(*lead):
    return pltpu.VMEM((*lead, 8, 128), jnp.float32)


def solve(parts):
    whole = field(4, 16)
    return pl.pallas_call(
        solve_kernel,
        out_shape=jax.ShapeDtypeStruct((64, 256), jnp.float32),
        scratch_shapes=[
            pltpu.VMEM((8, 64, 128), jnp.float32), pltpu.VMEM((64, 128), jnp.float32),
            whole, whole, whole, whole, field(3, 4, 16), whole, whole, whole, field(8), field(8),
        ],
        compiler_params=pltpu.CompilerParams(vmem_limit_bytes=40 * 1024 * 1024),
        name="solve",
    )(parts)


def on_device(right_side, links, coefs, reaction):
    message, order = pl.pallas_call(
        pack_kernel,
        out_shape=(jax.ShapeDtypeStruct((64, 384), jnp.float32), jax.ShapeDtypeStruct((128, 128), jnp.float32)),
        name="pack",
    )(right_side, links, coefs.reshape(1, 128), reaction.reshape(1, 128))
    received = lax.all_to_all(message, ("grp", "z"), 0, 0, tiled=True)
    along_x = lax.all_to_all(jnp.broadcast_to(received[None], (4, 64, 384)), "x", 0, 0, tiled=True)
    parts = lax.all_gather(along_x, "core", axis=0)
    answer = solve(parts)
    answer = lax.all_to_all(answer, ("grp", "z"), 0, 0, tiled=True)
    result, history = pl.pallas_call(
        unpack_kernel,
        out_shape=(jax.ShapeDtypeStruct((64, 128), jnp.float32), jax.ShapeDtypeStruct((8, 64), jnp.float32)),
        name="unpack",
    )(answer, order)
    return result, history[0:SWEEPS]


def solution(mesh):
    finer = Mesh(mesh.devices.reshape(8, 8, 4, 2), ("grp", "z", "x", "core"))
    blocks = ("grp", "z", "x", "core")
    return jax.shard_map(
        on_device,
        mesh=finer,
        in_specs=(P(None, blocks), P(None, blocks), P(blocks), P(blocks)),
        out_specs=(P(None, blocks), P()),
        check_vma=False,
    )
```

time: 482 us -> 95.8 us (0.20)
  starting transfers between devices: 132 us -> 0 us
  waiting for transfers between devices: 118 us -> 0 us
  blocking collectives: 137 us -> 58.6 us
  other arithmetic: 57.9 us -> 0 us
  Pallas kernels: 0 us -> 33.2 us
  local copies, waits for them, and re-layouts: 31.2 us -> 2.96 us
    psum x12 -> x0, blocking collectives: 137 us -> none  [over_axes(): return functools.reduce(lax.psum, axes, array)]
    ppermute x36 -> x0, starting transfers between devices: 132 us -> none  [shifted(): return lax.ppermute(block, axis, route)]
    ppermute x36 -> x0, waiting for transfers between devices: 118 us -> none  [shifted(): return lax.ppermute(block, axis, route)]
    scatter-add x9 -> x0, other arithmetic: 55 us -> none  [element_images(): return jnp.zeros_like(window).at[:, offsets].add(images)]
    all_to_all x0 -> x3, blocking collectives: none -> 53.1 us  [the longest x1 28.2 us: on_device(): received = lax.all_to_all(message, ('grp', 'z'), 0, 0, tiled=True)]
    pallas_call x0 -> x3, Pallas kernels: none -> 33.2 us  [the longest x1 29.5 us: solve(): pl.pallas_call(solve_kernel, out_shape=jax.ShapeDtypeStruct((64, 256), jn...]
    gather x18 -> x0, local copies, waits for them, and re-layouts: 27.1 us -> none  [element_images(): corners = window[:, offsets]]
    all_gather x0 -> x1, blocking collectives: none -> 5.51 us  [on_device(): parts = lax.all_gather(along_x, 'core', axis=0)]
  transfers between devices with their start and end apart: 36 -> 0, of which waited for: 36 -> 0; matrix products, arithmetic and copies ran while one was open for 0% -> 0% of each run, Pallas kernels for 0% -> 0%
where the time goes in v1:
time: 95.8 us; the launch traced here: 95.5 us
  blocking collectives  58.6 us (61%)
  Pallas kernels  33.2 us (35%)
  local copies, waits for them, and re-layouts  2.96 us (3%)
    pallas_call x1, Pallas kernels, solve(): pl.pallas_call(solve_kernel, out_shape=jax.ShapeDtypeStruct((64, 256), jn...  29.5 us
    all_to_all x1, blocking collectives, on_device(): received = lax.all_to_all(message, ('grp', 'z'), 0, 0, tiled=True)  28.2 us
    all_to_all x1, blocking collectives, on_device(): answer = lax.all_to_all(answer, ('grp', 'z'), 0, 0, tiled=True)  14.9 us
    all_to_all x1, blocking collectives, on_device(): lax.all_to_all(jnp.broadcast_to(received[None], (4, 64, 384)), 'x', 0, 0,...  10 us
    all_gather x1, blocking collectives, on_device(): parts = lax.all_gather(along_x, 'core', axis=0)  5.51 us
    pallas_call x1, Pallas kernels, on_device(): pl.pallas_call(pack_kernel, out_shape=(jax.ShapeDtypeStruct((64, 384), jn...  1.95 us

profile of v1, /device:TPU:1, one launch (start us, length us, event | category | flops | bytes accessed | tf_op | source)
XLA Modules:
  0.0 95.5 jit_solution(14375316980553974435)
XLA Ops:
  0.6 2.0 %pack.1 = (f32[64,384]{1,0:T(8,128)}, f32[128,128]{1,0:T(8,128)}) custom-call(f32[64,128]{1,0:T(8,128)} %right_ref.1, s32[8,128]{1,0:T(8,128)} %links_ref.1, f32[1,128]{1,0:T(1,128)} %bitcast.16, f32[1,128]{1,0:T(1,128)} %bitcast.17), custom_call_target="tpu_custom_call" | custom-call | tf_op jit(solution)/shard_map/pack/pallas_call | solution.py:256
  2.6 1.0 %copy.6 = f32[64,1,384]{2,1,0:T(1,128)S(1)} copy(f32[64,1,384]{2,0,1:T(8,128)} %bitcast.15) | data formatting | bytes 196608 | tf_op jit(solution)/shard_map/all_to_all | solution.py:261
  3.6 28.2 %all_to_all.25 = f32[64,1,384]{2,1,0:T(1,128)S(1)} all-to-all(f32[64,1,384]{2,1,0:T(1,128)S(1)} %copy.6), channel_id=1, replica_groups=mesh['grp'=8,'z'=8,'x'=4,'core'=2] {'grp','z'}, dimensions={0} | all-to-all | bytes 196608 | tf_op jit(solution)/shard_map/all_to_all | solution.py:261
  31.8 10.0 %all_to_all.26 = f32[4,64,384]{2,1,0:T(8,128)S(1)} all-to-all(f32[4,64,384]{2,1,0:T(8,128)S(1)} %broadcast_in_dim.9), channel_id=1, replica_groups=mesh['grp'=8,'z'=8,'x'=4,'core'=2] {'x'}, dimensions={0} | all-to-all | bytes 786432 | tf_op jit(solution)/shard_map/all_to_all | solution.py:262
  41.9 5.5 %all-gather = f32[8,64,384]{2,1,0:T(8,128)S(1)} all-gather(f32[4,64,384]{2,1,0:T(8,128)S(1)} %all_to_all.26), channel_id=2, replica_groups=mesh['grp'=8,'z'=8,'x'=4,'core'=2] {'core'}, dimensions={0}, use_global_device_ids=true | all-gather | bytes 1179648 | tf_op jit(solution)/shard_map/all_gather | solution.py:263
  47.4 29.5 %solve.1 = f32[64,256]{1,0:T(8,128)S(1)} custom-call(f32[2,4,64,384]{3,2,1,0:T(8,128)S(1)} %bitcast.11), custom_call_target="tpu_custom_call" | custom-call | tf_op jit(solution)/shard_map/solve/pallas_call | solution.py:243
  76.9 0.1 copy.7
  77.0 14.9 %all_to_all.27 = f32[64,1,256]{2,1,0:T(1,128)S(1)} all-to-all(f32[64,1,256]{2,1,0:T(1,128)S(1)} %copy.7), channel_id=1, replica_groups=mesh['grp'=8,'z'=8,'x'=4,'core'=2] {'grp','z'}, dimensions={0} | all-to-all | bytes 131072 | tf_op jit(solution)/shard_map/all_to_all | solution.py:265
  91.9 0.6 copy.13
  92.5 1.7 %unpack.1 = (f32[64,128]{1,0:T(8,128)}, f32[8,64]{1,0:T(8,128)}) custom-call(f32[64,256]{1,0:T(8,128)} %bitcast.14, f32[128,128]{1,0:T(8,128)} %get-tuple-element.7.order_ref), custom_call_target="tpu_custom_call" | custom-call | tf_op jit(solution)/shard_map/unpack/pallas_call | solution.py:266
  94.2 1.2 %slice.3 = f32[2,64]{1,0:T(2,128)} slice(f32[8,64]{1,0:T(8,128)} %get-tuple-element.9), slice={[0:2], [0:64]} | slice | bytes 1024 | tf_op jit(solution)/shard_map/slice | solution.py:271
  (2 shorter events, 0.0 us)

commit v2 on v1

--- a/solution.py
+++ b/solution.py
@@ -9,20 +9,36 @@
 SWEEPS = 2
 DEGREE = 4
 HIGHEST = lax.Precision.HIGHEST
+SMALL = pltpu.CompilerParams(vmem_limit_bytes=16 * 1024 * 1024)
 
 
 def dot(a, b, dims=((1,), (0,))):
     return lax.dot_general(a, b, (dims, ((), ())), precision=HIGHEST, preferred_element_type=jnp.float32)
 
 
-def pack_kernel(right_ref, links_ref, coefs_ref, reaction_ref, message_ref, order_ref):
+def orders_of(links_ref):
     row = lax.broadcasted_iota(jnp.int32, (128, 128), 0)
     lane = lax.broadcasted_iota(jnp.int32, (128, 128), 1)
-    regroup = (row == (lane % 8) * 16 + lane // 8).astype(jnp.float32)
-    slot = links_ref[0:1, :] & 127
-    onehot = (row == slot).astype(jnp.float32)
-    order = dot(onehot, regroup)
+    regroup = (row == (lane % 8) * 16 + lane // 8).astype(jnp.bfloat16)
+    onehot = (row == (links_ref[0:1, :] & 127)).astype(jnp.bfloat16)
+    order = jnp.dot(onehot, regroup, preferred_element_type=jnp.float32)
+    return regroup.astype(jnp.float32), order
+
+
+def pack_kernel(right_hbm, links_hbm, coefs_hbm, reaction_hbm, message_ref, order_ref, right_ref, links_ref, coefs_ref, reaction_ref, semaphores):
+    copies = [
+        pltpu.make_async_copy(source, target, semaphores.at[n])
+        for n, (source, target) in enumerate(
+            [(links_hbm, links_ref), (right_hbm, right_ref), (coefs_hbm, coefs_ref), (reaction_hbm, reaction_ref)]
+        )
+    ]
+    for copy in copies:
+        copy.start()
+    copies[0].wait()
+    regroup, order = orders_of(links_ref)
     order_ref[...] = order
+    for copy in copies[1:]:
+        copy.wait()
     message_ref[:, 0:128] = dot(right_ref[...], order)
     coefs = dot(jnp.broadcast_to(coefs_ref[...], (8, 128)), regroup)
     reaction = dot(jnp.broadcast_to(reaction_ref[...], (8, 128)), order)
@@ -33,7 +49,7 @@
 
 def unpack_kernel(message_ref, order_ref, solution_ref, history_ref):
     solution_ref[...] = dot(message_ref[:, 0:128], order_ref[...], ((1,), (1,)))
-    history_ref[...] = jnp.transpose(message_ref[:, 128:256])[0:8, :]
+    history_ref[...] = jnp.transpose(message_ref[:, 128:256])[0:SWEEPS, :]
 
 
 def exchange_lanes(tile):
@@ -48,9 +64,33 @@
     return tile
 
 
+def exchange_rows(tiles):
+    row = lax.broadcasted_iota(jnp.int32, (8, 128), 0)
+    tiles = list(tiles)
+    for bit in (1, 2, 4):
+        upper = (row & bit) != 0
+        for a in range(8):
+            if not a & bit:
+                b = a | bit
+                first, second = tiles[a], tiles[b]
+                tiles[a] = jnp.where(upper, pltpu.roll(second, bit, 0), first)
+                tiles[b] = jnp.where(upper, second, pltpu.roll(first, 8 - bit, 0))
+    return tiles
+
+
+def spread_kernel(message_ref, out_ref):
+    for kind in range(3):
+        tiles = [
+            exchange_lanes(message_ref[y * 8 : y * 8 + 8, kind * 128 : kind * 128 + 128]) for y in range(8)
+        ]
+        for ij, tile in enumerate(exchange_rows(tiles)):
+            for x in range(4):
+                out_ref[x, kind, ij] = tile
+
+
 def solve_kernel(
-    parts_ref, out_ref, regroup_ref, shift_ref, direct_ref, turned_ref, residual_ref, start_ref,
-    coef_ref, reaction_ref, minus_ref, plus_ref, correct_ref, solution_ref,
+    parts_ref, out_ref, direct_ref, turned_ref, residual_ref, start_ref, coef_ref, minus_ref, plus_ref,
+    correct_ref, solution_ref,
 ):
     lane = lax.broadcasted_iota(jnp.int32, (8, 128), 1)
     last_z = (lane & 7) == 7
@@ -71,24 +111,18 @@
 
     cells = [(i, w) for w in range(16) for i in range(4)]
 
-    for kind in range(3):
-        for x in range(4):
-            for core in range(2):
-                for y in range(8):
-                    tile = parts_ref[core, x, y * 8 : y * 8 + 8, kind * 128 : kind * 128 + 128]
-                    regroup_ref[x * 2 + core, y * 8 : y * 8 + 8, :] = exchange_lanes(tile)
-        for i, w in cells:
-            v = regroup_ref[w // 2, pl.ds(i * 2 + w % 2, 8, stride=8), :]
-            if kind == 0:
-                residual_ref[i, w] = v
-                direct_ref[i, w] = v
-                turned_ref[i, w] = next_k(v)
-            elif kind == 1:
-                coef_ref[0, i, w] = v * (1.0 / 16.0)
-                coef_ref[1, i, w] = v * (1.0 / 24.0)
-                coef_ref[2, i, w] = v * (1.0 / 48.0)
-            else:
-                reaction_ref[i, w] = v
+    def given(kind, i, w):
+        return parts_ref[w // 2 % 2, w // 4, kind, i * 2 + w % 2]
+
+    for i, w in cells:
+        v = given(0, i, w)
+        residual_ref[i, w] = v
+        direct_ref[i, w] = v
+        turned_ref[i, w] = next_k(v)
+        c = given(1, i, w)
+        coef_ref[0, i, w] = c * (1.0 / 16.0)
+        coef_ref[1, i, w] = c * (1.0 / 24.0)
+        coef_ref[2, i, w] = c * (1.0 / 48.0)
 
     def halves(v, shifted):
         return v + shifted, shifted - v
@@ -146,7 +180,7 @@
             plus_ref[i, 0] = s + d
 
     def image_of(i, w, v):
-        return minus_ref[i, w] + prev_k(plus_ref[i, w]) + reaction_ref[i, w] * v
+        return minus_ref[i, w] + prev_k(plus_ref[i, w]) + given(2, i, w) * v
 
     def over_all(v):
         return jnp.sum(jnp.sum(v, axis=1, keepdims=True), axis=0, keepdims=True)
@@ -227,10 +261,8 @@
         else:
             history = jnp.where(lane == sweep, rms, history)
 
-    for ij in range(8):
-        shift_ref[pl.ds(ij, 8, stride=8), :] = solution_ref[ij]
-    for y in range(8):
-        out_ref[y * 8 : y * 8 + 8, 0:128] = exchange_lanes(shift_ref[y * 8 : y * 8 + 8, :])
+    for y, tile in enumerate(exchange_rows([solution_ref[ij] for ij in range(8)])):
+        out_ref[y * 8 : y * 8 + 8, 0:128] = exchange_lanes(tile)
         out_ref[y * 8 : y * 8 + 8, 128:256] = history
 
 
@@ -244,10 +276,9 @@
         solve_kernel,
         out_shape=jax.ShapeDtypeStruct((64, 256), jnp.float32),
         scratch_shapes=[
-            pltpu.VMEM((8, 64, 128), jnp.float32), pltpu.VMEM((64, 128), jnp.float32),
-            whole, whole, whole, whole, field(3, 4, 16), whole, whole, whole, field(8), field(8),
+            whole, whole, whole, whole, field(3, 4, 16), whole, whole, field(8), field(8),
         ],
-        compiler_params=pltpu.CompilerParams(vmem_limit_bytes=40 * 1024 * 1024),
+        compiler_params=SMALL,
         name="solve",
     )(parts)
 
@@ -256,19 +287,30 @@
     message, order = pl.pallas_call(
         pack_kernel,
         out_shape=(jax.ShapeDtypeStruct((64, 384), jnp.float32), jax.ShapeDtypeStruct((128, 128), jnp.float32)),
+        in_specs=[pl.BlockSpec(memory_space=pltpu.HBM)] * 4,
+        scratch_shapes=[
+            pltpu.VMEM((64, 128), jnp.float32), pltpu.VMEM((8, 128), jnp.int32),
+            pltpu.VMEM((1, 128), jnp.float32), pltpu.VMEM((1, 128), jnp.float32), pltpu.SemaphoreType.DMA((4,)),
+        ],
+        compiler_params=SMALL,
         name="pack",
     )(right_side, links, coefs.reshape(1, 128), reaction.reshape(1, 128))
     received = lax.all_to_all(message, ("grp", "z"), 0, 0, tiled=True)
-    along_x = lax.all_to_all(jnp.broadcast_to(received[None], (4, 64, 384)), "x", 0, 0, tiled=True)
-    parts = lax.all_gather(along_x, "core", axis=0)
+    spread = pl.pallas_call(
+        spread_kernel,
+        out_shape=jax.ShapeDtypeStruct((4, 3, 8, 8, 128), jnp.float32),
+        compiler_params=SMALL,
+        name="spread",
+    )(received)
+    parts = lax.all_gather(lax.all_to_all(spread, "x", 0, 0, tiled=True), "core", axis=0)
     answer = solve(parts)
     answer = lax.all_to_all(answer, ("grp", "z"), 0, 0, tiled=True)
-    result, history = pl.pallas_call(
+    return pl.pallas_call(
         unpack_kernel,
-        out_shape=(jax.ShapeDtypeStruct((64, 128), jnp.float32), jax.ShapeDtypeStruct((8, 64), jnp.float32)),
+        out_shape=(jax.ShapeDtypeStruct((64, 128), jnp.float32), jax.ShapeDtypeStruct((SWEEPS, 64), jnp.float32)),
+        compiler_params=SMALL,
         name="unpack",
     )(answer, order)
-    return result, history[0:SWEEPS]
 
 
 def solution(mesh):

time: 95.8 us -> 69.9 us (0.73)
  Pallas kernels: 33.2 us -> 8 us
    pallas_call x1, Pallas kernels: 29.5 us -> 6.36 us  [solve(): pl.pallas_call(solve_kernel, out_shape=jax.ShapeDtypeStruct((64, 256), jn...]
    unnamed x2 -> x10, local copies, waits for them, and re-layouts: 0.62 us -> 2.11 us
    pallas_call x1, Pallas kernels: 1.95 us -> 0.51 us  [on_device(): pl.pallas_call(pack_kernel, out_shape=(jax.ShapeDtypeStruct((64, 384), jn...]
    slice x1 -> x0, local copies, waits for them, and re-layouts: 1.25 us -> none  [on_device(): return (result, history[0:SWEEPS])]
where the time goes in v2:
time: 69.9 us; the launch traced here: 69.6 us
  blocking collectives  58.6 us (84%)
  Pallas kernels  8 us (11%)
  local copies, waits for them, and re-layouts  2.28 us (3%)
    all_to_all x1, blocking collectives, on_device(): received = lax.all_to_all(message, ('grp', 'z'), 0, 0, tiled=True)  28.2 us
    all_to_all x1, blocking collectives, on_device(): answer = lax.all_to_all(answer, ('grp', 'z'), 0, 0, tiled=True)  14.9 us
    all_to_all x1, blocking collectives, on_device(): lax.all_to_all(spread, 'x', 0, 0, tiled=True)  10 us
    pallas_call x1, Pallas kernels, solve(): pl.pallas_call(solve_kernel, out_shape=jax.ShapeDtypeStruct((64, 256), jn...  6.36 us
    all_gather x1, blocking collectives, on_device(): lax.all_gather(lax.all_to_all(spread, 'x', 0, 0, tiled=True), 'core', axi...  5.51 us
    unnamed x10, local copies, waits for them, and re-layouts  2.11 us

profile of v2, /device:TPU:1, one launch (start us, length us, event | category | flops | bytes accessed | tf_op | source)
XLA Modules:
  0.0 69.6 jit_solution(10769423209566809608)
XLA Ops:
  0.6 0.0 copy-start.2
  0.6 0.0 copy-start.3
  0.7 0.6 copy-done.2
  1.3 0.0 copy-done.3
  1.3 0.0 copy-start
  1.3 0.8 %copy-done = f32[64,128]{1,0:T(8,128)S(1)} copy-done((f32[64,128]{1,0:T(8,128)S(1)}, f32[64,128]{1,0:T(8,128)}, u32[]{:S(2)}) %copy-start) | copy-done | bytes 32792
  2.1 0.0 copy-start.1
  2.1 0.7 copy-done.1
  2.7 0.5 pack.1
  3.3 0.1 copy.6
  3.4 28.2 %all_to_all.27 = f32[64,1,384]{2,1,0:T(1,128)S(1)} all-to-all(f32[64,1,384]{2,1,0:T(1,128)S(1)} %copy.6), channel_id=1, replica_groups=mesh['grp'=8,'z'=8,'x'=4,'core'=2] {'grp','z'}, dimensions={0} | all-to-all | bytes 196608 | tf_op jit(solution)/shard_map/all_to_all | solution.py:298
  31.6 0.3 spread.1
  31.9 10.0 %all_to_all.28 = f32[4,3,8,8,128]{4,3,2,1,0:T(8,128)S(1)} all-to-all(f32[4,3,8,8,128]{4,3,2,1,0:T(8,128)S(1)} %spread.1), channel_id=1, replica_groups=mesh['grp'=8,'z'=8,'x'=4,'core'=2] {'x'}, dimensions={0} | all-to-all | bytes 786432 | tf_op jit(solution)/shard_map/all_to_all | solution.py:305
  41.9 5.5 %all-gather = f32[8,3,8,8,128]{4,3,2,1,0:T(8,128)S(1)} all-gather(f32[4,3,8,8,128]{4,3,2,1,0:T(8,128)S(1)} %all_to_all.28), channel_id=2, replica_groups=mesh['grp'=8,'z'=8,'x'=4,'core'=2] {'core'}, dimensions={0}, use_global_device_ids=true | all-gather | bytes 1179648 | tf_op jit(solution)/shard_map/all_gather | solution.py:305
  47.4 6.4 %solve.1 = f32[64,256]{1,0:T(8,128)S(1)} custom-call(f32[2,4,3,8,8,128]{5,4,3,2,1,0:T(8,128)S(1)} %bitcast.11), custom_call_target="tpu_custom_call" | custom-call | tf_op jit(solution)/shard_map/solve/pallas_call | solution.py:275
  53.8 0.1 copy.7
  53.9 14.9 %all_to_all.29 = f32[64,1,256]{2,1,0:T(1,128)S(1)} all-to-all(f32[64,1,256]{2,1,0:T(1,128)S(1)} %copy.7), channel_id=1, replica_groups=mesh['grp'=8,'z'=8,'x'=4,'core'=2] {'grp','z'}, dimensions={0} | all-to-all | bytes 131072 | tf_op jit(solution)/shard_map/all_to_all | solution.py:307
  68.8 0.9 %unpack.1 = (f32[64,128]{1,0:T(8,128)}, f32[2,64]{1,0:T(2,128)}) custom-call(f32[64,256]{1,0:T(8,128)S(1)} %bitcast.13, f32[128,128]{1,0:T(8,128)S(1)} %get-tuple-element.5.order_ref), custom_call_target="tpu_custom_call" | custom-call | tf_op jit(solution)/shard_map/unpack/pallas_call | solution.py:308
  (2 shorter events, 0.0 us)
Async XLA Ops:
  0.6 0.7 copy-start.2
  0.6 0.7 copy-start.3
  1.3 0.8 %copy-start = (f32[64,128]{1,0:T(8,128)S(1)}, f32[64,128]{1,0:T(8,128)}, u32[]{:S(2)}) copy-start(f32[64,128]{1,0:T(8,128)} %right_hbm.1) | copy-start | bytes 98308
  2.1 0.7 copy-start.1

commit v3 on v2

--- a/solution.py
+++ b/solution.py
@@ -89,7 +89,7 @@
 
 
 def solve_kernel(
-    parts_ref, out_ref, direct_ref, turned_ref, residual_ref, start_ref, coef_ref, minus_ref, plus_ref,
+    parts_ref, out_ref, direct_ref, turned_ref, residual_ref, start_ref, coef_ref,
     correct_ref, solution_ref,
 ):
     lane = lax.broadcasted_iota(jnp.int32, (8, 128), 1)
@@ -114,87 +114,91 @@
     def given(kind, i, w):
         return parts_ref[w // 2 % 2, w // 4, kind, i * 2 + w % 2]
 
-    for i, w in cells:
-        v = given(0, i, w)
-        residual_ref[i, w] = v
-        direct_ref[i, w] = v
-        turned_ref[i, w] = next_k(v)
-        c = given(1, i, w)
-        coef_ref[0, i, w] = c * (1.0 / 16.0)
-        coef_ref[1, i, w] = c * (1.0 / 24.0)
-        coef_ref[2, i, w] = c * (1.0 / 48.0)
-
-    def halves(v, shifted):
-        return v + shifted, shifted - v
-
     def next_i(vs):
         return [vs[1], vs[2], vs[3], pltpu.roll(vs[0], 7, 0)]
 
     def prev_i(vs):
         return [pltpu.roll(vs[3], 1, 0), vs[0], vs[1], vs[2]]
 
-    def fold(minus_sum, sums):
-        return [m + s for m, s in zip(minus_sum, prev_i(sums))]
-
-    def apply_stiffness():
+    def mul(a, b):
+        return [p * q for p, q in zip(a, b)]
+
+    def add(a, b):
+        return [p + q for p, q in zip(a, b)]
+
+    def sub(a, b):
+        return [p - q for p, q in zip(a, b)]
+
+    for w in range(16):
+        below = [given(1, i, w) * (1.0 / 48.0) for i in range(4)]
+        both = add(below, prev_i(below))
+        for i in range(4):
+            v = given(0, i, w)
+            residual_ref[i, w] = v
+            direct_ref[i, w] = v
+            turned_ref[i, w] = next_k(v)
+            coef_ref[0, i, w] = below[i]
+            coef_ref[1, i, w] = below[i] * 3.0
+            coef_ref[2, i, w] = both[i] * 5.0
+            coef_ref[3, i, w] = both[i] * 3.0
+
+    def apply(visit):
         def load(w):
-            pairs = [halves(direct_ref[i, w], turned_ref[i, w]) for i in range(4)]
-            return [p[0] for p in pairs], [p[1] for p in pairs]
-
-        wrapped = []
-        for i in range(4):
-            v = next_z(direct_ref[i, 0])
-            wrapped.append(halves(v, next_k(v)))
-        wrapped = [p[0] for p in wrapped], [p[1] for p in wrapped]
+            here = [direct_ref[i, w] for i in range(4)]
+            turned = [turned_ref[i, w] for i in range(4)]
+            return add(here, turned), sub(turned, here)
+
+        def column(w, here, there):
+            coef = [[coef_ref[n, i, w] for i in range(4)] for n in range(4)]
+            lows, highs = [], []
+            for zk in range(2):
+                total, differ = add(here[zk], there[zk]), sub(there[zk], here[zk])
+                if zk == 0:
+                    flux = mul(coef[1], sub(next_i(total), total))
+                    total = sub(prev_i(flux), flux)
+                else:
+                    total = couple(coef[2], coef[0], total)
+                differ = couple(coef[2 + zk], coef[0], differ)
+                lows.append(sub(total, differ))
+                highs.append(add(total, differ))
+            return lows, highs
+
+        def couple(center, side, vs):
+            return add(add(mul(center, vs), mul(side, next_i(vs))), prev_i(mul(side, vs)))
+
+        def finish(w, totals):
+            for i in range(4):
+                total, differ = totals[0][i], totals[1][i]
+                v = direct_ref[i, w]
+                visit(i, w, v, ((total - differ) + given(2, i, w) * v) + prev_k(total + differ))
+
+        here = load(15)
+        wrapped = [next_z(direct_ref[i, 0]) for i in range(4)]
+        turned = [next_k(v) for v in wrapped]
+        kept, carry = column(15, here, (add(wrapped, turned), sub(turned, wrapped)))
+        carry = [[prev_z(v) for v in vs] for vs in carry]
+        last = here
         here = load(0)
-        carry = None
-        kept = None
-        for w in range(16):
-            there = load(w + 1) if w < 15 else wrapped
-            grads = []
-            for zk in range(2):
-                for yk in range(2):
-                    vs = [halves(a, b)[yk] for a, b in zip(here[zk], there[zk])]
-                    nexts = next_i(vs)
-                    differ = [(b - a) * coef_ref[zk + yk, i, w] for i, (a, b) in enumerate(zip(vs, nexts))]
-                    if zk + yk:
-                        total = [(a + b) * coef_ref[zk + yk - 1, i, w] for i, (a, b) in enumerate(zip(vs, nexts))]
-                        grads.append(fold([s - d for s, d in zip(total, differ)], [s + d for s, d in zip(total, differ)]))
-                    else:
-                        grads.append(fold([-d for d in differ], differ))
-            low = [[s - d for s, d in zip(grads[zk * 2], grads[zk * 2 + 1])] for zk in range(2)]
-            high = [[s + d for s, d in zip(grads[zk * 2], grads[zk * 2 + 1])] for zk in range(2)]
-            if w == 0:
-                kept = low
-            else:
-                low = [[a + b for a, b in zip(low[zk], carry[zk])] for zk in range(2)]
-                for i in range(4):
-                    minus_ref[i, w] = low[0][i] - low[1][i]
-                    plus_ref[i, w] = low[0][i] + low[1][i]
-            carry = high
-            here = there
-        for i in range(4):
-            s = kept[0][i] + prev_z(carry[0][i])
-            d = kept[1][i] + prev_z(carry[1][i])
-            minus_ref[i, 0] = s - d
-            plus_ref[i, 0] = s + d
-
-    def image_of(i, w, v):
-        return minus_ref[i, w] + prev_k(plus_ref[i, w]) + given(2, i, w) * v
+        for w in range(15):
+            there = load(w + 1) if w < 14 else last
+            low, high = column(w, here, there)
+            finish(w, [add(p, q) for p, q in zip(low, carry)])
+            carry, here = high, there
+        finish(15, [add(p, q) for p, q in zip(kept, carry)])
 
     def over_all(v):
         return jnp.sum(jnp.sum(v, axis=1, keepdims=True), axis=0, keepdims=True)
 
     zero = jnp.zeros((8, 128), jnp.float32)
 
-    apply_stiffness()
     crosses = [zero] * 4
     squares = [zero] * 4
-    for i, w in cells:
-        v = direct_ref[i, w]
-        image = image_of(i, w, v)
+
+    def measure(i, w, v, image):
         crosses[i] = crosses[i] + v * image
         squares[i] = squares[i] + image * image
+
+    apply(measure)
     cross = over_all((crosses[0] + crosses[1]) + (crosses[2] + crosses[3]))
     square = over_all((squares[0] + squares[1]) + (squares[2] + squares[3]))
     theta = square / cross
@@ -219,17 +223,18 @@
         def step(_, rho_now):
             for ij in range(8):
                 correct_ref[ij] = correct_ref[ij] + direct_ref[ij // 2, mine * 2 + ij % 2]
-            apply_stiffness()
             rho_next = 1.0 / (2.0 * sigma - rho_now)
             along = jnp.broadcast_to(rho_next * rho_now, (8, 128))
             across = jnp.broadcast_to(2.0 * rho_next / half, (8, 128))
-            for i, w in cells:
-                v = direct_ref[i, w]
-                r = residual_ref[i, w] - image_of(i, w, v)
+
+            def advance(i, w, v, image):
+                r = residual_ref[i, w] - image
                 residual_ref[i, w] = r
                 v = along * v + across * r
                 direct_ref[i, w] = v
                 turned_ref[i, w] = next_k(v)
+
+            apply(advance)
             return rho_next
 
         lax.fori_loop(0, DEGREE, step, 1.0 / sigma)
@@ -276,11 +281,15 @@
         solve_kernel,
         out_shape=jax.ShapeDtypeStruct((64, 256), jnp.float32),
         scratch_shapes=[
-            whole, whole, whole, whole, field(3, 4, 16), whole, whole, field(8), field(8),
+            whole, whole, whole, whole, field(4, 4, 16), field(8), field(8),
         ],
         compiler_params=SMALL,
         name="solve",
     )(parts)
+
+
+def in_hbm(array):
+    return pltpu.with_memory_space_constraint(array, pltpu.HBM)
 
 
 def on_device(right_side, links, coefs, reaction):
@@ -294,7 +303,7 @@
         ],
         compiler_params=SMALL,
         name="pack",
-    )(right_side, links, coefs.reshape(1, 128), reaction.reshape(1, 128))
+    )(*(in_hbm(a) for a in (right_side, links, coefs.reshape(1, 128), reaction.reshape(1, 128))))
     received = lax.all_to_all(message, ("grp", "z"), 0, 0, tiled=True)
     spread = pl.pallas_call(
         spread_kernel,

time: 69.9 us -> 67.5 us (0.966)
  local copies, waits for them, and re-layouts: 2.28 us -> 0.18 us
    unnamed x10 -> x2, local copies, waits for them, and re-layouts: 2.11 us -> 0.01 us
    pallas_call x1, Pallas kernels: 6.36 us -> 5.47 us  [solve(): pl.pallas_call(solve_kernel, out_shape=jax.ShapeDtypeStruct((64, 256), jn...]
where the time goes in v3:
time: 67.5 us; the launch traced here: 67.3 us
  blocking collectives  58.6 us (87%)
  Pallas kernels  7.78 us (12%)
  between operations  0.68 us (1%)
    all_to_all x1, blocking collectives, on_device(): received = lax.all_to_all(message, ('grp', 'z'), 0, 0, tiled=True)  28.2 us
    all_to_all x1, blocking collectives, on_device(): answer = lax.all_to_all(answer, ('grp', 'z'), 0, 0, tiled=True)  14.9 us
    all_to_all x1, blocking collectives, on_device(): lax.all_to_all(spread, 'x', 0, 0, tiled=True)  10 us
    all_gather x1, blocking collectives, on_device(): lax.all_gather(lax.all_to_all(spread, 'x', 0, 0, tiled=True), 'core', axi...  5.51 us
    pallas_call x1, Pallas kernels, solve(): pl.pallas_call(solve_kernel, out_shape=jax.ShapeDtypeStruct((64, 256), jn...  5.47 us

profile of v3, /device:TPU:1, one launch (start us, length us, event | category | flops | bytes accessed | tf_op | source)
XLA Modules:
  0.0 67.3 jit_solution(13772357496571191900)
XLA Ops:
  0.6 1.2 %pack.1 = (f32[64,384]{1,0:T(8,128)S(1)}, f32[128,128]{1,0:T(8,128)S(1)}) custom-call(f32[64,128]{1,0:T(8,128)} %right_hbm.1, s32[8,128]{1,0:T(8,128)} %links_hbm.1, f32[1,128]{1,0:T(1,128)} %bitcast.16, f32[1,128]{1,0:T(1,128)} %bitcast.17), custom_call_target="tpu_custom_call" | custom-call | tf_op jit(solution)/shard_map/pack/pallas_call | solution.py:296
  1.8 0.1 copy.6
  1.9 28.2 %all_to_all.27 = f32[64,1,384]{2,1,0:T(1,128)S(1)} all-to-all(f32[64,1,384]{2,1,0:T(1,128)S(1)} %copy.6), channel_id=1, replica_groups=mesh['grp'=8,'z'=8,'x'=4,'core'=2] {'grp','z'}, dimensions={0} | all-to-all | bytes 196608 | tf_op jit(solution)/shard_map/all_to_all | solution.py:307
  30.1 0.3 spread.1
  30.4 10.0 %all_to_all.28 = f32[4,3,8,8,128]{4,3,2,1,0:T(8,128)S(1)} all-to-all(f32[4,3,8,8,128]{4,3,2,1,0:T(8,128)S(1)} %spread.1), channel_id=1, replica_groups=mesh['grp'=8,'z'=8,'x'=4,'core'=2] {'x'}, dimensions={0} | all-to-all | bytes 786432 | tf_op jit(solution)/shard_map/all_to_all | solution.py:314
  40.4 5.5 %all-gather = f32[8,3,8,8,128]{4,3,2,1,0:T(8,128)S(1)} all-gather(f32[4,3,8,8,128]{4,3,2,1,0:T(8,128)S(1)} %all_to_all.28), channel_id=2, replica_groups=mesh['grp'=8,'z'=8,'x'=4,'core'=2] {'core'}, dimensions={0}, use_global_device_ids=true | all-gather | bytes 1179648 | tf_op jit(solution)/shard_map/all_gather | solution.py:314
  46.0 5.5 %solve.1 = f32[64,256]{1,0:T(8,128)S(1)} custom-call(f32[2,4,3,8,8,128]{5,4,3,2,1,0:T(8,128)S(1)} %bitcast.11), custom_call_target="tpu_custom_call" | custom-call | tf_op jit(solution)/shard_map/solve/pallas_call | solution.py:280
  51.4 0.1 copy.7
  51.5 14.9 %all_to_all.29 = f32[64,1,256]{2,1,0:T(1,128)S(1)} all-to-all(f32[64,1,256]{2,1,0:T(1,128)S(1)} %copy.7), channel_id=1, replica_groups=mesh['grp'=8,'z'=8,'x'=4,'core'=2] {'grp','z'}, dimensions={0} | all-to-all | bytes 131072 | tf_op jit(solution)/shard_map/all_to_all | solution.py:316
  66.4 0.9 %unpack.1 = (f32[64,128]{1,0:T(8,128)}, f32[2,64]{1,0:T(2,128)}) custom-call(f32[64,256]{1,0:T(8,128)S(1)} %bitcast.13, f32[128,128]{1,0:T(8,128)S(1)} %get-tuple-element.5.order_ref), custom_call_target="tpu_custom_call" | custom-call | tf_op jit(solution)/shard_map/unpack/pallas_call | solution.py:317
  (2 shorter events, 0.0 us)

commit v4 on v3

--- a/solution.py
+++ b/solution.py
@@ -90,7 +90,7 @@
 
 def solve_kernel(
     parts_ref, out_ref, direct_ref, turned_ref, residual_ref, start_ref, coef_ref,
-    correct_ref, solution_ref,
+    correct_ref,
 ):
     lane = lax.broadcasted_iota(jnp.int32, (8, 128), 1)
     last_z = (lane & 7) == 7
@@ -129,18 +129,24 @@
     def sub(a, b):
         return [p - q for p, q in zip(a, b)]
 
+    below = [[given(1, i, w) * (1.0 / 48.0) for i in range(4)] for w in range(16)]
+    both = [add(vs, prev_i(vs)) for vs in below]
     for w in range(16):
-        below = [given(1, i, w) * (1.0 / 48.0) for i in range(4)]
-        both = add(below, prev_i(below))
+        if w:
+            below_pair, both_pair = add(below[w], below[w - 1]), add(both[w], both[w - 1])
+        else:
+            below_pair = add(below[0], [prev_z(v) for v in below[15]])
+            both_pair = add(both[0], [prev_z(v) for v in both[15]])
         for i in range(4):
             v = given(0, i, w)
-            residual_ref[i, w] = v
             direct_ref[i, w] = v
             turned_ref[i, w] = next_k(v)
-            coef_ref[0, i, w] = below[i]
-            coef_ref[1, i, w] = below[i] * 3.0
-            coef_ref[2, i, w] = both[i] * 5.0
-            coef_ref[3, i, w] = both[i] * 3.0
+            coef_ref[0, i, w] = below[w][i]
+            coef_ref[1, i, w] = below[w][i] * 3.0
+            coef_ref[2, i, w] = both[w][i] * 5.0
+            coef_ref[3, i, w] = both[w][i] * 2.0
+            coef_ref[4, i, w] = below_pair[i] * 2.0
+            coef_ref[5, i, w] = both_pair[i] * 10.0
 
     def apply(visit):
         def load(w):
@@ -148,43 +154,38 @@
             turned = [turned_ref[i, w] for i in range(4)]
             return add(here, turned), sub(turned, here)
 
-        def column(w, here, there):
-            coef = [[coef_ref[n, i, w] for i in range(4)] for n in range(4)]
-            lows, highs = [], []
-            for zk in range(2):
-                total, differ = add(here[zk], there[zk]), sub(there[zk], here[zk])
-                if zk == 0:
-                    flux = mul(coef[1], sub(next_i(total), total))
-                    total = sub(prev_i(flux), flux)
-                else:
-                    total = couple(coef[2], coef[0], total)
-                differ = couple(coef[2 + zk], coef[0], differ)
-                lows.append(sub(total, differ))
-                highs.append(add(total, differ))
-            return lows, highs
+        def coef(n, w):
+            return [coef_ref[n, i, w] for i in range(4)]
 
         def couple(center, side, vs):
             return add(add(mul(center, vs), mul(side, next_i(vs))), prev_i(mul(side, vs)))
 
-        def finish(w, totals):
+        def column(w, here, there):
+            total, differ = add(here[0], there[0]), sub(there[0], here[0])
+            flux = mul(coef(1, w), sub(next_i(total), total))
+            total = sub(prev_i(flux), flux)
+            differ = couple(coef(2, w), coef(0, w), differ)
+            return sub(total, differ), add(total, differ), mul(coef(3, w), sub(there[1], here[1]))
+
+        def finish(w, here, now, before):
+            totals = add(now[0], before[1])
+            differs = add(couple(coef(5, w), coef(4, w), here[1]), sub(now[2], before[2]))
             for i in range(4):
-                total, differ = totals[0][i], totals[1][i]
                 v = direct_ref[i, w]
-                visit(i, w, v, ((total - differ) + given(2, i, w) * v) + prev_k(total + differ))
-
-        here = load(15)
+                visit(i, w, v, ((totals[i] - differs[i]) + given(2, i, w) * v) + prev_k(totals[i] + differs[i]))
+
+        first, last = load(0), load(15)
         wrapped = [next_z(direct_ref[i, 0]) for i in range(4)]
         turned = [next_k(v) for v in wrapped]
-        kept, carry = column(15, here, (add(wrapped, turned), sub(turned, wrapped)))
-        carry = [[prev_z(v) for v in vs] for vs in carry]
-        last = here
-        here = load(0)
+        kept = column(15, last, (add(wrapped, turned), sub(turned, wrapped)))
+        before = [[prev_z(v) for v in vs] for vs in kept]
+        here = first
         for w in range(15):
             there = load(w + 1) if w < 14 else last
-            low, high = column(w, here, there)
-            finish(w, [add(p, q) for p, q in zip(low, carry)])
-            carry, here = high, there
-        finish(15, [add(p, q) for p, q in zip(kept, carry)])
+            now = column(w, here, there)
+            finish(w, here, now, before)
+            here, before = there, now
+        finish(15, last, kept, before)
 
     def over_all(v):
         return jnp.sum(jnp.sum(v, axis=1, keepdims=True), axis=0, keepdims=True)
@@ -209,20 +210,25 @@
     sigma = center / half
     per_center = 1.0 / center
 
+    start_of = lambda i, w: given(0, i, w)
+    scale = jnp.broadcast_to(per_center, (8, 128))
+    for i, w in cells:
+        v = given(0, i, w) * scale
+        direct_ref[i, w] = v
+        turned_ref[i, w] = next_k(v)
+
     for sweep in range(SWEEPS):
-        scale = jnp.broadcast_to(per_center, (8, 128))
-        for i, w in cells:
-            r = residual_ref[i, w]
-            start_ref[i, w] = r
-            v = r * scale
-            direct_ref[i, w] = v
-            turned_ref[i, w] = next_k(v)
         for ij in range(8):
             correct_ref[ij] = zero
-
-        def step(_, rho_now):
+        for i, w in cells:
+            residual_ref[i, w] = start_of(i, w)
+
+        def correct():
             for ij in range(8):
                 correct_ref[ij] = correct_ref[ij] + direct_ref[ij // 2, mine * 2 + ij % 2]
+
+        def step(_, rho_now):
+            correct()
             rho_next = 1.0 / (2.0 * sigma - rho_now)
             along = jnp.broadcast_to(rho_next * rho_now, (8, 128))
             across = jnp.broadcast_to(2.0 * rho_next / half, (8, 128))
@@ -237,36 +243,44 @@
             apply(advance)
             return rho_next
 
-        lax.fori_loop(0, DEGREE, step, 1.0 / sigma)
+        lax.fori_loop(0, DEGREE - 1, step, 1.0 / sigma)
+        correct()
         crosses = [zero] * 4
         squares = [zero] * 4
-        for i, w in cells:
-            s = start_ref[i, w]
-            change = s - residual_ref[i, w]
+
+        def finish_sweep(i, w, v, image):
+            r = residual_ref[i, w] - image
+            residual_ref[i, w] = r
+            s = start_of(i, w)
+            change = s - r
             crosses[i] = crosses[i] + s * change
             squares[i] = squares[i] + change * change
+
+        apply(finish_sweep)
         along = over_all((crosses[0] + crosses[1]) + (crosses[2] + crosses[3]))
         length = over_all((squares[0] + squares[1]) + (squares[2] + squares[3]))
         omega = jnp.broadcast_to(along / length, (8, 128))
         squares = [zero] * 4
         for i, w in cells:
-            s = start_ref[i, w]
+            s = start_of(i, w)
             r = s - omega * (s - residual_ref[i, w])
-            residual_ref[i, w] = r
             squares[i] = squares[i] + r * r
-        for ij in range(8):
-            if sweep == 0:
-                solution_ref[ij] = omega * correct_ref[ij]
-            else:
-                solution_ref[ij] = solution_ref[ij] + omega * correct_ref[ij]
+            if sweep < SWEEPS - 1:
+                start_ref[i, w] = r
+                v = r * scale
+                direct_ref[i, w] = v
+                turned_ref[i, w] = next_k(v)
+        start_of = lambda i, w: start_ref[i, w]
         total = over_all((squares[0] + squares[1]) + (squares[2] + squares[3]))
         rms = jnp.broadcast_to(jnp.sqrt(total / 65536.0), (8, 128))
         if sweep == 0:
             history = rms
+            answer = [omega * correct_ref[ij] for ij in range(8)]
         else:
             history = jnp.where(lane == sweep, rms, history)
-
-    for y, tile in enumerate(exchange_rows([solution_ref[ij] for ij in range(8)])):
+            answer = [a + omega * correct_ref[ij] for ij, a in enumerate(answer)]
+
+    for y, tile in enumerate(exchange_rows(answer)):
         out_ref[y * 8 : y * 8 + 8, 0:128] = exchange_lanes(tile)
         out_ref[y * 8 : y * 8 + 8, 128:256] = history
 
@@ -281,7 +295,7 @@
         solve_kernel,
         out_shape=jax.ShapeDtypeStruct((64, 256), jnp.float32),
         scratch_shapes=[
-            whole, whole, whole, whole, field(4, 4, 16), field(8), field(8),
+            whole, whole, whole, whole, field(6, 4, 16), field(8),
         ],
         compiler_params=SMALL,
         name="solve",

time: 67.5 us -> 66.9 us (level)
  no operation moved by 1% of the time
where the time goes in v4:
time: 66.9 us; the launch traced here: 66.7 us
  blocking collectives  58.6 us (88%)
  Pallas kernels  7.16 us (11%)
  between operations  0.68 us (1%)
    all_to_all x1, blocking collectives, on_device(): received = lax.all_to_all(message, ('grp', 'z'), 0, 0, tiled=True)  28.2 us
    all_to_all x1, blocking collectives, on_device(): answer = lax.all_to_all(answer, ('grp', 'z'), 0, 0, tiled=True)  14.9 us
    all_to_all x1, blocking collectives, on_device(): lax.all_to_all(spread, 'x', 0, 0, tiled=True)  10 us
    all_gather x1, blocking collectives, on_device(): lax.all_gather(lax.all_to_all(spread, 'x', 0, 0, tiled=True), 'core', axi...  5.51 us
    pallas_call x1, Pallas kernels, solve(): pl.pallas_call(solve_kernel, out_shape=jax.ShapeDtypeStruct((64, 256), jn...  4.86 us

profile of v4, /device:TPU:1, one launch (start us, length us, event | category | flops | bytes accessed | tf_op | source)
XLA Modules:
  0.0 66.7 jit_solution(11614987625345734343)
XLA Ops:
  0.6 1.2 %pack.1 = (f32[64,384]{1,0:T(8,128)S(1)}, f32[128,128]{1,0:T(8,128)S(1)}) custom-call(f32[64,128]{1,0:T(8,128)} %right_hbm.1, s32[8,128]{1,0:T(8,128)} %links_hbm.1, f32[1,128]{1,0:T(1,128)} %bitcast.16, f32[1,128]{1,0:T(1,128)} %bitcast.17), custom_call_target="tpu_custom_call" | custom-call | tf_op jit(solution)/shard_map/pack/pallas_call | solution.py:310
  1.8 0.1 copy.6
  1.9 28.2 %all_to_all.27 = f32[64,1,384]{2,1,0:T(1,128)S(1)} all-to-all(f32[64,1,384]{2,1,0:T(1,128)S(1)} %copy.6), channel_id=1, replica_groups=mesh['grp'=8,'z'=8,'x'=4,'core'=2] {'grp','z'}, dimensions={0} | all-to-all | bytes 196608 | tf_op jit(solution)/shard_map/all_to_all | solution.py:321
  30.1 0.3 spread.1
  30.4 10.0 %all_to_all.28 = f32[4,3,8,8,128]{4,3,2,1,0:T(8,128)S(1)} all-to-all(f32[4,3,8,8,128]{4,3,2,1,0:T(8,128)S(1)} %spread.1), channel_id=1, replica_groups=mesh['grp'=8,'z'=8,'x'=4,'core'=2] {'x'}, dimensions={0} | all-to-all | bytes 786432 | tf_op jit(solution)/shard_map/all_to_all | solution.py:328
  40.4 5.5 %all-gather = f32[8,3,8,8,128]{4,3,2,1,0:T(8,128)S(1)} all-gather(f32[4,3,8,8,128]{4,3,2,1,0:T(8,128)S(1)} %all_to_all.28), channel_id=2, replica_groups=mesh['grp'=8,'z'=8,'x'=4,'core'=2] {'core'}, dimensions={0}, use_global_device_ids=true | all-gather | bytes 1179648 | tf_op jit(solution)/shard_map/all_gather | solution.py:328
  46.0 4.9 %solve.1 = f32[64,256]{1,0:T(8,128)S(1)} custom-call(f32[2,4,3,8,8,128]{5,4,3,2,1,0:T(8,128)S(1)} %bitcast.11), custom_call_target="tpu_custom_call" | custom-call | tf_op jit(solution)/shard_map/solve/pallas_call | solution.py:294
  50.8 0.1 copy.7
  50.9 14.9 %all_to_all.29 = f32[64,1,256]{2,1,0:T(1,128)S(1)} all-to-all(f32[64,1,256]{2,1,0:T(1,128)S(1)} %copy.7), channel_id=1, replica_groups=mesh['grp'=8,'z'=8,'x'=4,'core'=2] {'grp','z'}, dimensions={0} | all-to-all | bytes 131072 | tf_op jit(solution)/shard_map/all_to_all | solution.py:330
  65.8 0.9 %unpack.1 = (f32[64,128]{1,0:T(8,128)}, f32[2,64]{1,0:T(2,128)}) custom-call(f32[64,256]{1,0:T(8,128)S(1)} %bitcast.13, f32[128,128]{1,0:T(8,128)S(1)} %get-tuple-element.5.order_ref), custom_call_target="tpu_custom_call" | custom-call | tf_op jit(solution)/shard_map/unpack/pallas_call | solution.py:331
  (2 shorter events, 0.0 us)

commit v5 on v4

--- a/solution.py
+++ b/solution.py
@@ -8,6 +8,8 @@
 
 SWEEPS = 2
 DEGREE = 4
+EARLY = 5
+LATE = (13, 14, 15)
 HIGHEST = lax.Precision.HIGHEST
 SMALL = pltpu.CompilerParams(vmem_limit_bytes=16 * 1024 * 1024)
 
@@ -138,9 +140,6 @@
             below_pair = add(below[0], [prev_z(v) for v in below[15]])
             both_pair = add(both[0], [prev_z(v) for v in both[15]])
         for i in range(4):
-            v = given(0, i, w)
-            direct_ref[i, w] = v
-            turned_ref[i, w] = next_k(v)
             coef_ref[0, i, w] = below[w][i]
             coef_ref[1, i, w] = below[w][i] * 3.0
             coef_ref[2, i, w] = both[w][i] * 5.0
@@ -148,10 +147,15 @@
             coef_ref[4, i, w] = below_pair[i] * 2.0
             coef_ref[5, i, w] = both_pair[i] * 10.0
 
-    def apply(visit):
+    def save(i, w, v):
+        direct_ref[i, w] = v
+        if w not in LATE:
+            turned_ref[i, w] = next_k(v)
+
+    def apply(visit, of=lambda i, w: direct_ref[i, w], turned_of=lambda i, w: turned_ref[i, w]):
         def load(w):
-            here = [direct_ref[i, w] for i in range(4)]
-            turned = [turned_ref[i, w] for i in range(4)]
+            here = [of(i, w) for i in range(4)]
+            turned = [next_k(here[i]) if w in LATE else turned_of(i, w) for i in range(4)]
             return add(here, turned), sub(turned, here)
 
         def coef(n, w):
@@ -171,21 +175,22 @@
             totals = add(now[0], before[1])
             differs = add(couple(coef(5, w), coef(4, w), here[1]), sub(now[2], before[2]))
             for i in range(4):
-                v = direct_ref[i, w]
+                v = of(i, w)
                 visit(i, w, v, ((totals[i] - differs[i]) + given(2, i, w) * v) + prev_k(totals[i] + differs[i]))
 
-        first, last = load(0), load(15)
-        wrapped = [next_z(direct_ref[i, 0]) for i in range(4)]
+        wrapped = [next_z(of(i, 0)) for i in range(4)]
         turned = [next_k(v) for v in wrapped]
-        kept = column(15, last, (add(wrapped, turned), sub(turned, wrapped)))
-        before = [[prev_z(v) for v in vs] for vs in kept]
-        here = first
-        for w in range(15):
-            there = load(w + 1) if w < 14 else last
-            now = column(w, here, there)
-            finish(w, here, now, before)
-            here, before = there, now
-        finish(15, last, kept, before)
+        nodes = [load(w) for w in range(16)] + [(add(wrapped, turned), sub(turned, wrapped))]
+        made = {}
+        for w in (*range(EARLY), 15, *range(EARLY, 15)):
+            made[w] = column(w, nodes[w], nodes[w + 1])
+            if w == 15:
+                made[-1] = [[prev_z(v) for v in vs] for vs in made[15]]
+                for early in range(EARLY):
+                    finish(early, nodes[early], made[early], made[early - 1])
+            elif w >= EARLY:
+                finish(w, nodes[w], made[w], made[w - 1])
+        finish(15, nodes[15], made[15], made[14])
 
     def over_all(v):
         return jnp.sum(jnp.sum(v, axis=1, keepdims=True), axis=0, keepdims=True)
@@ -198,8 +203,9 @@
     def measure(i, w, v, image):
         crosses[i] = crosses[i] + v * image
         squares[i] = squares[i] + image * image
-
-    apply(measure)
+        start_ref[i, w] = image
+
+    apply(measure, lambda i, w: given(0, i, w), lambda i, w: next_k(given(0, i, w)))
     cross = over_all((crosses[0] + crosses[1]) + (crosses[2] + crosses[3]))
     square = over_all((squares[0] + squares[1]) + (squares[2] + squares[3]))
     theta = square / cross
@@ -210,18 +216,27 @@
     sigma = center / half
     per_center = 1.0 / center
 
+    def advanced(rho_now):
+        rho_next = 1.0 / (2.0 * sigma - rho_now)
+        return rho_next, jnp.broadcast_to(rho_next * rho_now, (8, 128)), jnp.broadcast_to(2.0 * rho_next / half, (8, 128))
+
     start_of = lambda i, w: given(0, i, w)
     scale = jnp.broadcast_to(per_center, (8, 128))
+    rho_first, along, across = advanced(1.0 / sigma)
     for i, w in cells:
-        v = given(0, i, w) * scale
-        direct_ref[i, w] = v
-        turned_ref[i, w] = next_k(v)
+        s = start_of(i, w)
+        r = s - start_ref[i, w] * scale
+        residual_ref[i, w] = r
+        save(i, w, along * (s * scale) + across * r)
+    for ij in range(8):
+        correct_ref[ij] = parts_ref[lax.axis_index("core"), lax.axis_index("x"), 0, ij] * scale
 
     for sweep in range(SWEEPS):
-        for ij in range(8):
-            correct_ref[ij] = zero
-        for i, w in cells:
-            residual_ref[i, w] = start_of(i, w)
+        if sweep:
+            for ij in range(8):
+                correct_ref[ij] = zero
+            for i, w in cells:
+                residual_ref[i, w] = start_of(i, w)
 
         def correct():
             for ij in range(8):
@@ -229,21 +244,20 @@
 
         def step(_, rho_now):
             correct()
-            rho_next = 1.0 / (2.0 * sigma - rho_now)
-            along = jnp.broadcast_to(rho_next * rho_now, (8, 128))
-            across = jnp.broadcast_to(2.0 * rho_next / half, (8, 128))
+            rho_next, along, across = advanced(rho_now)
 
             def advance(i, w, v, image):
                 r = residual_ref[i, w] - image
                 residual_ref[i, w] = r
-                v = along * v + across * r
-                direct_ref[i, w] = v
-                turned_ref[i, w] = next_k(v)
+                save(i, w, along * v + across * r)
 
             apply(advance)
             return rho_next
 
-        lax.fori_loop(0, DEGREE - 1, step, 1.0 / sigma)
+        if sweep:
+            lax.fori_loop(0, DEGREE - 1, step, 1.0 / sigma)
+        else:
+            lax.fori_loop(1, DEGREE - 1, step, rho_first)
         correct()
         crosses = [zero] * 4
         squares = [zero] * 4
@@ -267,9 +281,7 @@
             squares[i] = squares[i] + r * r
             if sweep < SWEEPS - 1:
                 start_ref[i, w] = r
-                v = r * scale
-                direct_ref[i, w] = v
-                turned_ref[i, w] = next_k(v)
+                save(i, w, r * scale)
         start_of = lambda i, w: start_ref[i, w]
         total = over_all((squares[0] + squares[1]) + (squares[2] + squares[3]))
         rms = jnp.broadcast_to(jnp.sqrt(total / 65536.0), (8, 128))

time: 66.9 us -> 66.4 us (level)
  no operation moved by 1% of the time
where the time goes in v5:
time: 66.4 us; the launch traced here: 66.1 us
  blocking collectives  58.6 us (88%)
  Pallas kernels  6.62 us (10%)
  between operations  0.68 us (1%)
    all_to_all x1, blocking collectives, on_device(): received = lax.all_to_all(message, ('grp', 'z'), 0, 0, tiled=True)  28.2 us
    all_to_all x1, blocking collectives, on_device(): answer = lax.all_to_all(answer, ('grp', 'z'), 0, 0, tiled=True)  14.9 us
    all_to_all x1, blocking collectives, on_device(): lax.all_to_all(spread, 'x', 0, 0, tiled=True)  10 us
    all_gather x1, blocking collectives, on_device(): lax.all_gather(lax.all_to_all(spread, 'x', 0, 0, tiled=True), 'core', axi...  5.51 us
    pallas_call x1, Pallas kernels, solve(): pl.pallas_call(solve_kernel, out_shape=jax.ShapeDtypeStruct((64, 256), jn...  4.32 us

profile of v5, /device:TPU:1, one launch (start us, length us, event | category | flops | bytes accessed | tf_op | source)
XLA Modules:
  0.0 66.1 jit_solution(4853762261270704650)
XLA Ops:
  0.6 1.2 %pack.1 = (f32[64,384]{1,0:T(8,128)S(1)}, f32[128,128]{1,0:T(8,128)S(1)}) custom-call(f32[64,128]{1,0:T(8,128)} %right_hbm.1, s32[8,128]{1,0:T(8,128)} %links_hbm.1, f32[1,128]{1,0:T(1,128)} %bitcast.16, f32[1,128]{1,0:T(1,128)} %bitcast.17), custom_call_target="tpu_custom_call" | custom-call | tf_op jit(solution)/shard_map/pack/pallas_call | solution.py:322
  1.8 0.1 copy.6
  1.9 28.2 %all_to_all.27 = f32[64,1,384]{2,1,0:T(1,128)S(1)} all-to-all(f32[64,1,384]{2,1,0:T(1,128)S(1)} %copy.6), channel_id=1, replica_groups=mesh['grp'=8,'z'=8,'x'=4,'core'=2] {'grp','z'}, dimensions={0} | all-to-all | bytes 196608 | tf_op jit(solution)/shard_map/all_to_all | solution.py:333
  30.1 0.3 spread.1
  30.4 10.0 %all_to_all.28 = f32[4,3,8,8,128]{4,3,2,1,0:T(8,128)S(1)} all-to-all(f32[4,3,8,8,128]{4,3,2,1,0:T(8,128)S(1)} %spread.1), channel_id=1, replica_groups=mesh['grp'=8,'z'=8,'x'=4,'core'=2] {'x'}, dimensions={0} | all-to-all | bytes 786432 | tf_op jit(solution)/shard_map/all_to_all | solution.py:340
  40.4 5.5 %all-gather = f32[8,3,8,8,128]{4,3,2,1,0:T(8,128)S(1)} all-gather(f32[4,3,8,8,128]{4,3,2,1,0:T(8,128)S(1)} %all_to_all.28), channel_id=2, replica_groups=mesh['grp'=8,'z'=8,'x'=4,'core'=2] {'core'}, dimensions={0}, use_global_device_ids=true | all-gather | bytes 1179648 | tf_op jit(solution)/shard_map/all_gather | solution.py:340
  46.0 4.3 %solve.1 = f32[64,256]{1,0:T(8,128)S(1)} custom-call(f32[2,4,3,8,8,128]{5,4,3,2,1,0:T(8,128)S(1)} %bitcast.11), custom_call_target="tpu_custom_call" | custom-call | tf_op jit(solution)/shard_map/solve/pallas_call | solution.py:306
  50.3 0.1 copy.7
  50.4 14.9 %all_to_all.29 = f32[64,1,256]{2,1,0:T(1,128)S(1)} all-to-all(f32[64,1,256]{2,1,0:T(1,128)S(1)} %copy.7), channel_id=1, replica_groups=mesh['grp'=8,'z'=8,'x'=4,'core'=2] {'grp','z'}, dimensions={0} | all-to-all | bytes 131072 | tf_op jit(solution)/shard_map/all_to_all | solution.py:342
  65.3 0.9 %unpack.1 = (f32[64,128]{1,0:T(8,128)}, f32[2,64]{1,0:T(2,128)}) custom-call(f32[64,256]{1,0:T(8,128)S(1)} %bitcast.13, f32[128,128]{1,0:T(8,128)S(1)} %get-tuple-element.5.order_ref), custom_call_target="tpu_custom_call" | custom-call | tf_op jit(solution)/shard_map/unpack/pallas_call | solution.py:343
  (2 shorter events, 0.0 us)

commit v6 on v5

--- a/solution.py
+++ b/solution.py
@@ -8,14 +8,27 @@
 
 SWEEPS = 2
 DEGREE = 4
+CENTER = (1.5 + 0.15) / 2.0
+HALF = (1.5 - 0.15) / 2.0
+RHOS = [HALF / CENTER]
+for _ in range(DEGREE - 1):
+    RHOS.append(1.0 / (2.0 * CENTER / HALF - RHOS[-1]))
 EARLY = 5
 LATE = (13, 14, 15)
-HIGHEST = lax.Precision.HIGHEST
 SMALL = pltpu.CompilerParams(vmem_limit_bytes=16 * 1024 * 1024)
 
 
-def dot(a, b, dims=((1,), (0,))):
-    return lax.dot_general(a, b, (dims, ((), ())), precision=HIGHEST, preferred_element_type=jnp.float32)
+def pick(values, onehot, dims=((1,), (0,))):
+    rows = values.shape[0]
+    high = values.astype(jnp.bfloat16)
+    rest = values - high.astype(jnp.float32)
+    middle = rest.astype(jnp.bfloat16)
+    low = (rest - middle.astype(jnp.float32)).astype(jnp.bfloat16)
+    parts = [
+        lax.dot_general(part, onehot, (dims, ((), ())), preferred_element_type=jnp.float32)
+        for part in (high, middle, low)
+    ]
+    return (parts[2] + parts[1]) + parts[0]
 
 
 def orders_of(links_ref):
@@ -24,7 +37,7 @@
     regroup = (row == (lane % 8) * 16 + lane // 8).astype(jnp.bfloat16)
     onehot = (row == (links_ref[0:1, :] & 127)).astype(jnp.bfloat16)
     order = jnp.dot(onehot, regroup, preferred_element_type=jnp.float32)
-    return regroup.astype(jnp.float32), order
+    return regroup, order.astype(jnp.bfloat16)
 
 
 def pack_kernel(right_hbm, links_hbm, coefs_hbm, reaction_hbm, message_ref, order_ref, right_ref, links_ref, coefs_ref, reaction_ref, semaphores):
@@ -41,16 +54,16 @@
     order_ref[...] = order
     for copy in copies[1:]:
         copy.wait()
-    message_ref[:, 0:128] = dot(right_ref[...], order)
-    coefs = dot(jnp.broadcast_to(coefs_ref[...], (8, 128)), regroup)
-    reaction = dot(jnp.broadcast_to(reaction_ref[...], (8, 128)), order)
+    message_ref[:, 0:128] = pick(right_ref[...], order)
+    coefs = pick(jnp.broadcast_to(coefs_ref[...], (8, 128)), regroup)
+    reaction = pick(jnp.broadcast_to(reaction_ref[...], (8, 128)), order)
     for block in range(8):
         message_ref[block * 8 : block * 8 + 8, 128:256] = coefs
         message_ref[block * 8 : block * 8 + 8, 256:384] = reaction
 
 
 def unpack_kernel(message_ref, order_ref, solution_ref, history_ref):
-    solution_ref[...] = dot(message_ref[:, 0:128], order_ref[...], ((1,), (1,)))
+    solution_ref[...] = pick(message_ref[:, 0:128], order_ref[...], ((1,), (1,)))
     history_ref[...] = jnp.transpose(message_ref[:, 128:256])[0:SWEEPS, :]
 
 
@@ -208,21 +221,19 @@
     apply(measure, lambda i, w: given(0, i, w), lambda i, w: next_k(given(0, i, w)))
     cross = over_all((crosses[0] + crosses[1]) + (crosses[2] + crosses[3]))
     square = over_all((squares[0] + squares[1]) + (squares[2] + squares[3]))
-    theta = square / cross
-    upper = 1.5 * theta
-    lower = upper / 10.0
-    center = (upper + lower) / 2.0
-    half = (upper - lower) / 2.0
-    sigma = center / half
-    per_center = 1.0 / center
-
-    def advanced(rho_now):
-        rho_next = 1.0 / (2.0 * sigma - rho_now)
-        return rho_next, jnp.broadcast_to(rho_next * rho_now, (8, 128)), jnp.broadcast_to(2.0 * rho_next / half, (8, 128))
+    per_theta = cross / square
+
+    def advanced(step):
+        kept, added = RHOS[1] * RHOS[0], 2.0 * RHOS[1] / HALF
+        if not isinstance(step, int) or step:
+            for n in range(1, DEGREE - 1):
+                kept = jnp.where(step == n, RHOS[n + 1] * RHOS[n], kept)
+                added = jnp.where(step == n, 2.0 * RHOS[n + 1] / HALF, added)
+        return kept, jnp.broadcast_to(added * per_theta, (8, 128))
 
     start_of = lambda i, w: given(0, i, w)
-    scale = jnp.broadcast_to(per_center, (8, 128))
-    rho_first, along, across = advanced(1.0 / sigma)
+    scale = jnp.broadcast_to(per_theta * (1.0 / CENTER), (8, 128))
+    along, across = advanced(0)
     for i, w in cells:
         s = start_of(i, w)
         r = s - start_ref[i, w] * scale
@@ -242,9 +253,9 @@
             for ij in range(8):
                 correct_ref[ij] = correct_ref[ij] + direct_ref[ij // 2, mine * 2 + ij % 2]
 
-        def step(_, rho_now):
+        def step(number, carry):
             correct()
-            rho_next, along, across = advanced(rho_now)
+            along, across = advanced(number)
 
             def advance(i, w, v, image):
                 r = residual_ref[i, w] - image
@@ -252,12 +263,9 @@
                 save(i, w, along * v + across * r)
 
             apply(advance)
-            return rho_next
-
-        if sweep:
-            lax.fori_loop(0, DEGREE - 1, step, 1.0 / sigma)
-        else:
-            lax.fori_loop(1, DEGREE - 1, step, rho_first)
+            return carry
+
+        lax.fori_loop(0 if sweep else 1, DEGREE - 1, step, 0)
         correct()
         crosses = [zero] * 4
         squares = [zero] * 4
@@ -321,7 +329,7 @@
 def on_device(right_side, links, coefs, reaction):
     message, order = pl.pallas_call(
         pack_kernel,
-        out_shape=(jax.ShapeDtypeStruct((64, 384), jnp.float32), jax.ShapeDtypeStruct((128, 128), jnp.float32)),
+        out_shape=(jax.ShapeDtypeStruct((64, 384), jnp.float32), jax.ShapeDtypeStruct((128, 128), jnp.bfloat16)),
         in_specs=[pl.BlockSpec(memory_space=pltpu.HBM)] * 4,
         scratch_shapes=[
             pltpu.VMEM((64, 128), jnp.float32), pltpu.VMEM((8, 128), jnp.int32),

time: 66.4 us -> 66.3 us (level)
  no operation moved by 1% of the time
where the time goes in v6:
time: 66.3 us; the launch traced here: 66 us
  blocking collectives  58.6 us (88%)
  Pallas kernels  6.49 us (10%)
  between operations  0.68 us (1%)
    all_to_all x1, blocking collectives, on_device(): received = lax.all_to_all(message, ('grp', 'z'), 0, 0, tiled=True)  28.2 us
    all_to_all x1, blocking collectives, on_device(): answer = lax.all_to_all(answer, ('grp', 'z'), 0, 0, tiled=True)  14.9 us
    all_to_all x1, blocking collectives, on_device(): lax.all_to_all(spread, 'x', 0, 0, tiled=True)  10 us
    all_gather x1, blocking collectives, on_device(): lax.all_gather(lax.all_to_all(spread, 'x', 0, 0, tiled=True), 'core', axi...  5.51 us
    pallas_call x1, Pallas kernels, solve(): pl.pallas_call(solve_kernel, out_shape=jax.ShapeDtypeStruct((64, 256), jn...  4.33 us

profile of v6, /device:TPU:1, one launch (start us, length us, event | category | flops | bytes accessed | tf_op | source)
XLA Modules:
  0.0 66.0 jit_solution(2672526995063517138)
XLA Ops:
  0.6 1.1 %pack.1 = (f32[64,384]{1,0:T(8,128)S(1)}, bf16[128,128]{1,0:T(8,128)(2,1)S(1)}) custom-call(f32[64,128]{1,0:T(8,128)} %right_hbm.1, s32[8,128]{1,0:T(8,128)} %links_hbm.1, f32[1,128]{1,0:T(1,128)} %bitcast.16, f32[1,128]{1,0:T(1,128)} %bitcast.17), custom_call_target="tpu_custom_call" | custom-call | tf_op jit(solution)/shard_map/pack/pallas_call | solution.py:330
  1.7 0.1 copy.6
  1.8 28.2 %all_to_all.27 = f32[64,1,384]{2,1,0:T(1,128)S(1)} all-to-all(f32[64,1,384]{2,1,0:T(1,128)S(1)} %copy.6), channel_id=1, replica_groups=mesh['grp'=8,'z'=8,'x'=4,'core'=2] {'grp','z'}, dimensions={0} | all-to-all | bytes 196608 | tf_op jit(solution)/shard_map/all_to_all | solution.py:341
  30.0 0.3 spread.1
  30.3 10.0 %all_to_all.28 = f32[4,3,8,8,128]{4,3,2,1,0:T(8,128)S(1)} all-to-all(f32[4,3,8,8,128]{4,3,2,1,0:T(8,128)S(1)} %spread.1), channel_id=1, replica_groups=mesh['grp'=8,'z'=8,'x'=4,'core'=2] {'x'}, dimensions={0} | all-to-all | bytes 786432 | tf_op jit(solution)/shard_map/all_to_all | solution.py:348
  40.4 5.5 %all-gather = f32[8,3,8,8,128]{4,3,2,1,0:T(8,128)S(1)} all-gather(f32[4,3,8,8,128]{4,3,2,1,0:T(8,128)S(1)} %all_to_all.28), channel_id=2, replica_groups=mesh['grp'=8,'z'=8,'x'=4,'core'=2] {'core'}, dimensions={0}, use_global_device_ids=true | all-gather | bytes 1179648 | tf_op jit(solution)/shard_map/all_gather | solution.py:348
  45.9 4.3 %solve.1 = f32[64,256]{1,0:T(8,128)S(1)} custom-call(f32[2,4,3,8,8,128]{5,4,3,2,1,0:T(8,128)S(1)} %bitcast.11), custom_call_target="tpu_custom_call" | custom-call | tf_op jit(solution)/shard_map/solve/pallas_call | solution.py:314
  50.2 0.1 copy.7
  50.3 14.9 %all_to_all.29 = f32[64,1,256]{2,1,0:T(1,128)S(1)} all-to-all(f32[64,1,256]{2,1,0:T(1,128)S(1)} %copy.7), channel_id=1, replica_groups=mesh['grp'=8,'z'=8,'x'=4,'core'=2] {'grp','z'}, dimensions={0} | all-to-all | bytes 131072 | tf_op jit(solution)/shard_map/all_to_all | solution.py:350
  65.2 0.8 %unpack.1 = (f32[64,128]{1,0:T(8,128)}, f32[2,64]{1,0:T(2,128)}) custom-call(f32[64,256]{1,0:T(8,128)S(1)} %bitcast.13, bf16[128,128]{1,0:T(8,128)(2,1)S(1)} %get-tuple-element.5.order_ref), custom_call_target="tpu_custom_call" | custom-call | tf_op jit(solution)/shard_map/unpack/pallas_call | solution.py:351
  (2 shorter events, 0.0 us)

commit v7 on v6

--- a/solution.py
+++ b/solution.py
@@ -31,13 +31,8 @@
     return (parts[2] + parts[1]) + parts[0]
 
 
-def orders_of(links_ref):
-    row = lax.broadcasted_iota(jnp.int32, (128, 128), 0)
-    lane = lax.broadcasted_iota(jnp.int32, (128, 128), 1)
-    regroup = (row == (lane % 8) * 16 + lane // 8).astype(jnp.bfloat16)
-    onehot = (row == (links_ref[0:1, :] & 127)).astype(jnp.bfloat16)
-    order = jnp.dot(onehot, regroup, preferred_element_type=jnp.float32)
-    return regroup, order.astype(jnp.bfloat16)
+def gather_lanes(values, lanes):
+    return jnp.take_along_axis(values, jnp.broadcast_to(lanes[0:1], values.shape), axis=1, mode="promise_in_bounds")
 
 
 def pack_kernel(right_hbm, links_hbm, coefs_hbm, reaction_hbm, message_ref, order_ref, right_ref, links_ref, coefs_ref, reaction_ref, semaphores):
@@ -50,13 +45,16 @@
     for copy in copies:
         copy.start()
     copies[0].wait()
-    regroup, order = orders_of(links_ref)
-    order_ref[...] = order
+    lane = lax.broadcasted_iota(jnp.int32, (8, 128), 1)
+    element = (lane & 7) * 16 + (lane >> 3)
+    slot = gather_lanes(jnp.broadcast_to(links_ref[0:1, :] & 127, (8, 128)), element)
+    row = lax.broadcasted_iota(jnp.int32, (128, 128), 0)
+    order_ref[...] = (row == slot[0:1]).astype(jnp.float32).astype(jnp.bfloat16)
     for copy in copies[1:]:
         copy.wait()
-    message_ref[:, 0:128] = pick(right_ref[...], order)
-    coefs = pick(jnp.broadcast_to(coefs_ref[...], (8, 128)), regroup)
-    reaction = pick(jnp.broadcast_to(reaction_ref[...], (8, 128)), order)
+    message_ref[:, 0:128] = gather_lanes(right_ref[...], slot)
+    coefs = gather_lanes(jnp.broadcast_to(coefs_ref[...], (8, 128)), element)
+    reaction = gather_lanes(jnp.broadcast_to(reaction_ref[...], (8, 128)), slot)
     for block in range(8):
         message_ref[block * 8 : block * 8 + 8, 128:256] = coefs
         message_ref[block * 8 : block * 8 + 8, 256:384] = reaction

time: 66.3 us -> 66.1 us (level)
  no operation moved by 1% of the time
where the time goes in v7:
time: 66.1 us; the launch traced here: 65.8 us
  blocking collectives  58.6 us (89%)
  Pallas kernels  6.3 us (10%)
  between operations  0.68 us (1%)
    all_to_all x1, blocking collectives, on_device(): received = lax.all_to_all(message, ('grp', 'z'), 0, 0, tiled=True)  28.2 us
    all_to_all x1, blocking collectives, on_device(): answer = lax.all_to_all(answer, ('grp', 'z'), 0, 0, tiled=True)  14.9 us
    all_to_all x1, blocking collectives, on_device(): lax.all_to_all(spread, 'x', 0, 0, tiled=True)  10 us
    all_gather x1, blocking collectives, on_device(): lax.all_gather(lax.all_to_all(spread, 'x', 0, 0, tiled=True), 'core', axi...  5.51 us
    pallas_call x1, Pallas kernels, solve(): pl.pallas_call(solve_kernel, out_shape=jax.ShapeDtypeStruct((64, 256), jn...  4.33 us

profile of v7, /device:TPU:1, one launch (start us, length us, event | category | flops | bytes accessed | tf_op | source)
XLA Modules:
  0.0 65.8 jit_solution(16534004454108466568)
XLA Ops:
  0.6 0.9 %pack.1 = (f32[64,384]{1,0:T(8,128)S(1)}, bf16[128,128]{1,0:T(8,128)(2,1)S(1)}) custom-call(f32[64,128]{1,0:T(8,128)} %right_hbm.1, s32[8,128]{1,0:T(8,128)} %links_hbm.1, f32[1,128]{1,0:T(1,128)} %bitcast.16, f32[1,128]{1,0:T(1,128)} %bitcast.17), custom_call_target="tpu_custom_call" | custom-call | tf_op jit(solution)/shard_map/pack/pallas_call | solution.py:328
  1.5 0.1 copy.6
  1.6 28.2 %all_to_all.27 = f32[64,1,384]{2,1,0:T(1,128)S(1)} all-to-all(f32[64,1,384]{2,1,0:T(1,128)S(1)} %copy.6), channel_id=1, replica_groups=mesh['grp'=8,'z'=8,'x'=4,'core'=2] {'grp','z'}, dimensions={0} | all-to-all | bytes 196608 | tf_op jit(solution)/shard_map/all_to_all | solution.py:339
  29.8 0.3 spread.1
  30.1 10.0 %all_to_all.28 = f32[4,3,8,8,128]{4,3,2,1,0:T(8,128)S(1)} all-to-all(f32[4,3,8,8,128]{4,3,2,1,0:T(8,128)S(1)} %spread.1), channel_id=1, replica_groups=mesh['grp'=8,'z'=8,'x'=4,'core'=2] {'x'}, dimensions={0} | all-to-all | bytes 786432 | tf_op jit(solution)/shard_map/all_to_all | solution.py:346
  40.2 5.5 %all-gather = f32[8,3,8,8,128]{4,3,2,1,0:T(8,128)S(1)} all-gather(f32[4,3,8,8,128]{4,3,2,1,0:T(8,128)S(1)} %all_to_all.28), channel_id=2, replica_groups=mesh['grp'=8,'z'=8,'x'=4,'core'=2] {'core'}, dimensions={0}, use_global_device_ids=true | all-gather | bytes 1179648 | tf_op jit(solution)/shard_map/all_gather | solution.py:346
  45.7 4.3 %solve.1 = f32[64,256]{1,0:T(8,128)S(1)} custom-call(f32[2,4,3,8,8,128]{5,4,3,2,1,0:T(8,128)S(1)} %bitcast.11), custom_call_target="tpu_custom_call" | custom-call | tf_op jit(solution)/shard_map/solve/pallas_call | solution.py:312
  50.0 0.1 copy.7
  50.1 14.9 %all_to_all.29 = f32[64,1,256]{2,1,0:T(1,128)S(1)} all-to-all(f32[64,1,256]{2,1,0:T(1,128)S(1)} %copy.7), channel_id=1, replica_groups=mesh['grp'=8,'z'=8,'x'=4,'core'=2] {'grp','z'}, dimensions={0} | all-to-all | bytes 131072 | tf_op jit(solution)/shard_map/all_to_all | solution.py:348
  65.0 0.8 %unpack.1 = (f32[64,128]{1,0:T(8,128)}, f32[2,64]{1,0:T(2,128)}) custom-call(f32[64,256]{1,0:T(8,128)S(1)} %bitcast.13, bf16[128,128]{1,0:T(8,128)(2,1)S(1)} %get-tuple-element.5.order_ref), custom_call_target="tpu_custom_call" | custom-call | tf_op jit(solution)/shard_map/unpack/pallas_call | solution.py:349
  (2 shorter events, 0.0 us)

commit v8 on v7

--- a/solution.py
+++ b/solution.py
@@ -52,12 +52,12 @@
     order_ref[...] = (row == slot[0:1]).astype(jnp.float32).astype(jnp.bfloat16)
     for copy in copies[1:]:
         copy.wait()
-    message_ref[:, 0:128] = gather_lanes(right_ref[...], slot)
+    message_ref[:, 0, 0:128] = gather_lanes(right_ref[...], slot)
     coefs = gather_lanes(jnp.broadcast_to(coefs_ref[...], (8, 128)), element)
     reaction = gather_lanes(jnp.broadcast_to(reaction_ref[...], (8, 128)), slot)
     for block in range(8):
-        message_ref[block * 8 : block * 8 + 8, 128:256] = coefs
-        message_ref[block * 8 : block * 8 + 8, 256:384] = reaction
+        message_ref[block * 8 : block * 8 + 8, 0, 128:256] = coefs
+        message_ref[block * 8 : block * 8 + 8, 0, 256:384] = reaction
 
 
 def unpack_kernel(message_ref, order_ref, solution_ref, history_ref):
@@ -299,8 +299,8 @@
             answer = [a + omega * correct_ref[ij] for ij, a in enumerate(answer)]
 
     for y, tile in enumerate(exchange_rows(answer)):
-        out_ref[y * 8 : y * 8 + 8, 0:128] = exchange_lanes(tile)
-        out_ref[y * 8 : y * 8 + 8, 128:256] = history
+        out_ref[y * 8 : y * 8 + 8, 0, 0:128] = exchange_lanes(tile)
+        out_ref[y * 8 : y * 8 + 8, 0, 128:256] = history
 
 
 def field(*lead):
@@ -311,7 +311,7 @@
     whole = field(4, 16)
     return pl.pallas_call(
         solve_kernel,
-        out_shape=jax.ShapeDtypeStruct((64, 256), jnp.float32),
+        out_shape=jax.ShapeDtypeStruct((64, 1, 256), jnp.float32),
         scratch_shapes=[
             whole, whole, whole, whole, field(6, 4, 16), field(8),
         ],
@@ -327,7 +327,7 @@
 def on_device(right_side, links, coefs, reaction):
     message, order = pl.pallas_call(
         pack_kernel,
-        out_shape=(jax.ShapeDtypeStruct((64, 384), jnp.float32), jax.ShapeDtypeStruct((128, 128), jnp.bfloat16)),
+        out_shape=(jax.ShapeDtypeStruct((64, 1, 384), jnp.float32), jax.ShapeDtypeStruct((128, 128), jnp.bfloat16)),
         in_specs=[pl.BlockSpec(memory_space=pltpu.HBM)] * 4,
         scratch_shapes=[
             pltpu.VMEM((64, 128), jnp.float32), pltpu.VMEM((8, 128), jnp.int32),
@@ -342,7 +342,7 @@
         out_shape=jax.ShapeDtypeStruct((4, 3, 8, 8, 128), jnp.float32),
         compiler_params=SMALL,
         name="spread",
-    )(received)
+    )(received.reshape(64, 384))
     parts = lax.all_gather(lax.all_to_all(spread, "x", 0, 0, tiled=True), "core", axis=0)
     answer = solve(parts)
     answer = lax.all_to_all(answer, ("grp", "z"), 0, 0, tiled=True)
@@ -351,7 +351,7 @@
         out_shape=(jax.ShapeDtypeStruct((64, 128), jnp.float32), jax.ShapeDtypeStruct((SWEEPS, 64), jnp.float32)),
         compiler_params=SMALL,
         name="unpack",
-    )(answer, order)
+    )(answer.reshape(64, 256), order)
 
 
 def solution(mesh):

time: 66.1 us -> 65.9 us (level)
  no operation moved by 1% of the time
where the time goes in v8:
time: 65.9 us; the launch traced here: 65.7 us
  blocking collectives  58.6 us (89%)
  Pallas kernels  6.35 us (10%)
  between operations  0.66 us (1%)
    all_to_all x1, blocking collectives, on_device(): received = lax.all_to_all(message, ('grp', 'z'), 0, 0, tiled=True)  28.2 us
    all_to_all x1, blocking collectives, on_device(): answer = lax.all_to_all(answer, ('grp', 'z'), 0, 0, tiled=True)  14.9 us
    all_to_all x1, blocking collectives, on_device(): lax.all_to_all(spread, 'x', 0, 0, tiled=True)  10 us
    all_gather x1, blocking collectives, on_device(): lax.all_gather(lax.all_to_all(spread, 'x', 0, 0, tiled=True), 'core', axi...  5.51 us
    pallas_call x1, Pallas kernels, solve(): pl.pallas_call(solve_kernel, out_shape=jax.ShapeDtypeStruct((64, 1, 256),...  4.33 us

profile of v8, /device:TPU:1, one launch (start us, length us, event | category | flops | bytes accessed | tf_op | source)
XLA Modules:
  0.0 65.7 jit_solution(9363521807110761320)
XLA Ops:
  0.6 0.9 %pack.1 = (f32[64,1,384]{2,1,0:T(1,128)S(1)}, bf16[128,128]{1,0:T(8,128)(2,1)S(1)}) custom-call(f32[64,128]{1,0:T(8,128)} %right_hbm.1, s32[8,128]{1,0:T(8,128)} %links_hbm.1, f32[1,128]{1,0:T(1,128)} %bitcast.12, f32[1,128]{1,0:T(1,128)} %bitcast.13), custom_call_target="tpu_custom_call" | custom-call | tf_op jit(solution)/shard_map/pack/pallas_call | solution.py:328
  1.6 28.2 %all_to_all.15 = f32[64,1,384]{2,1,0:T(1,128)S(1)} all-to-all(f32[64,1,384]{2,1,0:T(1,128)S(1)} %get-tuple-element.4), channel_id=1, replica_groups=mesh['grp'=8,'z'=8,'x'=4,'core'=2] {'grp','z'}, dimensions={0} | all-to-all | bytes 196608 | tf_op jit(solution)/shard_map/all_to_all | solution.py:339
  29.8 0.3 spread.1
  30.1 10.0 %all_to_all.16 = f32[4,3,8,8,128]{4,3,2,1,0:T(8,128)S(1)} all-to-all(f32[4,3,8,8,128]{4,3,2,1,0:T(8,128)S(1)} %spread.1), channel_id=1, replica_groups=mesh['grp'=8,'z'=8,'x'=4,'core'=2] {'x'}, dimensions={0} | all-to-all | bytes 786432 | tf_op jit(solution)/shard_map/all_to_all | solution.py:346
  40.1 5.5 %all-gather = f32[8,3,8,8,128]{4,3,2,1,0:T(8,128)S(1)} all-gather(f32[4,3,8,8,128]{4,3,2,1,0:T(8,128)S(1)} %all_to_all.16), channel_id=2, replica_groups=mesh['grp'=8,'z'=8,'x'=4,'core'=2] {'core'}, dimensions={0}, use_global_device_ids=true | all-gather | bytes 1179648 | tf_op jit(solution)/shard_map/all_gather | solution.py:346
  45.6 4.3 %solve.1 = f32[64,1,256]{2,1,0:T(1,128)S(1)} custom-call(f32[2,4,3,8,8,128]{5,4,3,2,1,0:T(8,128)S(1)} %bitcast.9), custom_call_target="tpu_custom_call" | custom-call | tf_op jit(solution)/shard_map/solve/pallas_call | solution.py:312
  50.0 14.9 %all_to_all.17 = f32[64,1,256]{2,1,0:T(1,128)S(1)} all-to-all(f32[64,1,256]{2,1,0:T(1,128)S(1)} %solve.1), channel_id=1, replica_groups=mesh['grp'=8,'z'=8,'x'=4,'core'=2] {'grp','z'}, dimensions={0} | all-to-all | bytes 131072 | tf_op jit(solution)/shard_map/all_to_all | solution.py:348
  64.8 0.8 %unpack.1 = (f32[64,128]{1,0:T(8,128)}, f32[2,64]{1,0:T(2,128)}) custom-call(f32[64,256]{1,0:T(8,128)S(1)} %bitcast.11, bf16[128,128]{1,0:T(8,128)(2,1)S(1)} %get-tuple-element.5.order_ref), custom_call_target="tpu_custom_call" | custom-call | tf_op jit(solution)/shard_map/unpack/pallas_call | solution.py:349
  (2 shorter events, 0.0 us)
